TPU v7x, 512 devices: a whole 4x8x8 slice. The times are simulated.
512 devices in a mesh: cuts: 32 (over z, y_hi, core), row: 16 (over x, y_lo).
Axes of the slice: x: 4, y: 8 (y_hi: 2, y_lo: 4; y = y_hi * 4 + y_lo), z: 8, core: 2. Of those that a mesh axis runs over, the one named last changes fastest.
Arguments:
- propagator: float32 [8192, 8192], P('row', 'cuts'), as said below
- slab: float32 [8192, 256], P('cuts', 'row'), may hold values from -6 to 6
- fields: int32 [4, 8192], replicated, may hold values from 0 to 1
- phonon: int32 [4, 8192], replicated, may hold values from 0 to 15
- couplings: float32 [16], replicated, may hold values from -0.6 to 0.6
Outputs:
- updated: float32 [8192, 256], P('cuts', 'row')
Inputs may be any that keep to these rules, and one draw needn't show every extreme that they name: propagator is symmetric.
All inputs are finite; a program needn't handle non-finite values.
Results may differ from a plain program's by a relative error of at most 0.00011.
Values sent between devices are 32-bit elements; how exact they have to be, the bound alone decides.
No kernel may reach another device: no remote copies, remote signals or barrier semaphores. Data moves between devices by JAX's collectives and lax.ppermute only.
A program may use at most 64 MiB of HBM per device.

v0:
```python
import jax
import jax.numpy as jnp
from jax import lax
from jax.sharding import PartitionSpec as P

SITES = 8192
SLICES = 4


hs_strength = 0.3


def extended(cells, sides, width):
    for axis, dim in sides:
        count = lax.axis_size(axis)
        head = lax.slice_in_dim(cells, 0, width, axis=dim)
        tail = lax.slice_in_dim(cells, cells.shape[dim] - width, cells.shape[dim], axis=dim)
        cells = jnp.concatenate(
            [
                lax.ppermute(tail, axis, [(i, (i + 1) % count) for i in range(count)]),
                cells,
                lax.ppermute(head, axis, [((i + 1) % count, i) for i in range(count)]),
            ],
            axis=dim,
        )
    return cells


def from_everyone(x, axis):
    peers = lax.axis_size(axis)
    return lax.all_to_all(jnp.broadcast_to(x[None], (peers, *x.shape)), axis, 0, 0, tiled=True)


def laid_out(parts, dim):
    parts = jnp.moveaxis(parts, 0, dim)
    lengths = parts.shape
    return parts.reshape(*lengths[:dim], lengths[dim] * lengths[dim + 1], *lengths[dim + 2 :])


def gather_directly(x, axis, dim):
    parts = from_everyone(x, axis)
    return laid_out(parts, dim)


def in_blocks(x, dim, peers):
    lengths = x.shape
    parts = x.reshape(*lengths[:dim], peers, lengths[dim] // peers, *lengths[dim + 1 :])
    return jnp.moveaxis(parts, dim, 0)


def sent_and_summed(x, axis, dim):
    parts = in_blocks(x, dim, lax.axis_size(axis))
    arrived = lax.all_to_all(parts, axis, split_axis=0, concat_axis=0, tiled=True)
    return arrived.sum(axis=0)


def lookup(indices, couplings):
    levels = jnp.arange(couplings.shape[0], dtype=jnp.int32)
    hits = indices[:, None] == levels[None, :]
    return jnp.sum(jnp.where(hits, couplings[None, :], 0.0), axis=1)


def apply_bonds(shares, first_site, slice_no, fields, phonon, couplings, rim):
    count = shares.shape[0]
    level_row = phonon[slice_no]
    window = lax.dynamic_slice_in_dim(level_row, first_site, count)
    before = lax.dynamic_slice_in_dim(level_row, (first_site - 1 + SITES) % SITES, 1)
    parity = jnp.arange(count, dtype=jnp.int32) % 2
    even_bonds = jnp.repeat(window[0::2], 2)
    odd_bonds = jnp.where(parity == 1, window, jnp.concatenate([before, window[:-1]]))
    even_rate = lookup(even_bonds, couplings)[:, None]
    odd_rate = lookup(odd_bonds, couplings)[:, None]
    partner = shares.reshape(count // 2, 2, shares.shape[1])[:, ::-1].reshape(shares.shape)
    mixed = jnp.cosh(even_rate) * shares + jnp.sinh(even_rate) * partner
    padded = rim(mixed)
    partner = jnp.where(parity[:, None] == 0, padded[:-2], padded[2:])
    mixed = jnp.cosh(odd_rate) * mixed + jnp.sinh(odd_rate) * partner
    field_row = lax.dynamic_slice_in_dim(fields[slice_no], first_site, count)
    signs = (2 * field_row - 1).astype(jnp.float32)
    return jnp.exp(hs_strength * signs)[:, None] * mixed


def rim_cols_even(mixed):
    return extended(mixed, (("row", 0),), 1)


def rim_cols_odd(mixed):
    return extended(mixed, (("cuts", 0),), 1)


def shards(propagator, slab, fields, phonon, couplings):
    cut_index = lax.axis_index("cuts")
    row_index = lax.axis_index("row")
    current = slab
    for slice_no in range(SLICES):
        if slice_no % 2 == 0:
            summed = jnp.dot(
                propagator,
                gather_directly(current, "row", 1),
                precision=lax.Precision.HIGHEST,
                preferred_element_type=jnp.float32,
            )
            shares = sent_and_summed(summed, "cuts", 1)
            first_site = row_index * shares.shape[0]
            current = apply_bonds(
                shares, first_site, slice_no, fields, phonon, couplings, rim_cols_even
            )
        else:
            summed = lax.dot_general(
                propagator,
                gather_directly(current, "cuts", 1),
                (((0,), (0,)), ((), ())),
                precision=lax.Precision.HIGHEST,
                preferred_element_type=jnp.float32,
            )
            shares = sent_and_summed(summed, "row", 1)
            first_site = cut_index * shares.shape[0]
            current = apply_bonds(
                shares, first_site, slice_no, fields, phonon, couplings, rim_cols_odd
            )
    return current


def solution(mesh):
    in_specs = (P("row", "cuts"), P("cuts", "row"), P(), P(), P())
    out_specs = P("cuts", "row")
    return jax.shard_map(shards, mesh=mesh, in_specs=in_specs, out_specs=out_specs, check_vma=False)
```

profile of v0, /device:TPU:1, one launch (start us, length us, event | category | flops | bytes accessed | tf_op | source)
XLA Modules:
  0.0 238.2 jit_solution(9703148361331127402)
XLA Ops:
  0.0 1.5 broadcast_in_dim.154
  1.5 8.1 %all-to-all-start = ((f32[16,256,16]{1,2,0:T(8,128)}), f32[16,256,16]{1,2,0:T(8,128)S(1)}, u32[]{:S(2)}, u32[]{:S(2)}) async-start(f32[16,256,16]{1,2,0:T(8,128)} %broadcast_in_dim.154), calls=%async_computation | async-start | bytes 524288 | tf_op jit(solution)/shard_map/all_to_all | solution.py:31
  9.7 0.1 fusion.55
  9.8 0.8 copy-done.2
  10.6 0.1 fusion.56
  10.8 6.9 %all-to-all-done = f32[16,256,16]{1,2,0:T(8,128)S(1)} async-done(((f32[16,256,16]{1,2,0:T(8,128)}), f32[16,256,16]{1,2,0:T(8,128)S(1)}, u32[]{:S(2)}, u32[]{:S(2)}) %all-to-all-start) | async-done | bytes 262176 | tf_op jit(solution)/shard_map/all_to_all | solution.py:31
  17.6 0.7 convolution_bitcast_fusion.1
  18.3 1.1 copy.28
  19.4 16.9 %all-to-all-start.1 = ((f32[32,512,8]{1,2,0:T(8,128)}), f32[32,512,8]{1,2,0:T(8,128)S(1)}, u32[]{:S(2)}, u32[]{:S(2)}) async-start(f32[32,512,8]{1,2,0:T(8,128)} %copy.28), calls=%async_computation.1 | async-start | bytes 1048576 | tf_op jit(solution)/shard_map/all_to_all | solution.py:53
  36.3 0.2 slice.123
  36.6 0.2 slice.115
  36.8 0.1 broadcast_in_dim.151
  36.9 0.1 eq.183
  37.1 0.1 eq.197
  37.3 0.6 constant_dynamic-slice_fusion.4
  37.9 0.6 constant_dynamic-slice_fusion.10
  38.5 0.7 add_select_fusion.2
  39.2 0.7 add_select_fusion.1
  39.9 0.1 select_reduce_fusion.3
  40.1 13.9 %all-to-all-done.1 = f32[32,512,8]{1,2,0:T(8,128)S(1)} async-done(((f32[32,512,8]{1,2,0:T(8,128)}), f32[32,512,8]{1,2,0:T(8,128)S(1)}, u32[]{:S(2)}, u32[]{:S(2)}) %all-to-all-start.1) | async-done | bytes 524320 | tf_op jit(solution)/shard_map/all_to_all | solution.py:53
  54.0 0.1 copy.30
  54.2 0.6 rev.12
  54.8 0.1 copy.31
  55.0 4.6 %collective-permute-start = (f32[1,8]{0,1:T(8,128)S(1)}, f32[1,8]{0,1:T(8,128)S(1)}, u32[]{:S(2)}, u32[]{:S(2)}) collective-permute-start(f32[1,8]{0,1:T(8,128)S(1)} %get-tuple-element.27), channel_id=1, source_target_pairs={{0,1},{1,2},{2,3},{3,4},{4,5},{5,6},{6,7},{7,8},{8,9},{9,10},{10,1... | collective-permute-start | bytes 104 | tf_op jit(solution)/shard_map/ppermute | solution.py:20
  59.6 4.6 %collective-permute-start.1 = (f32[1,8]{0,1:T(8,128)S(1)}, f32[1,8]{0,1:T(8,128)S(1)}, u32[]{:S(2)}, u32[]{:S(2)}) collective-permute-start(f32[1,8]{0,1:T(8,128)S(1)} %get-tuple-element.28), channel_id=1, source_target_pairs={{1,0},{2,1},{3,2},{4,3},{5,4},{6,5},{7,6},{8,7},{9,8},{10,9},{11,1... | collective-permute-start | bytes 104 | tf_op jit(solution)/shard_map/ppermute | solution.py:22
  64.2 0.7 collective-permute-done.1
  65.0 0.9 broadcast_in_dim.156
  65.9 8.5 %all-to-all-start.2 = ((f32[32,512,8]{1,2,0:T(8,128)}), f32[32,512,8]{1,2,0:T(8,128)S(1)}, u32[]{:S(2)}, u32[]{:S(2)}) async-start(f32[32,512,8]{1,2,0:T(8,128)} %broadcast_in_dim.156), calls=%async_computation.2 | async-start | bytes 1048576 | tf_op jit(solution)/shard_map/all_to_all | solution.py:31
  74.4 0.2 slice.119
  74.6 0.2 slice.111
  74.9 0.2 eq.175
  75.2 0.2 eq.190
  75.4 0.7 add_select_fusion.4
  76.1 0.6 add_select_fusion.3
  76.8 0.1 select_reduce_fusion.7
  76.9 14.5 %all-to-all-done.2 = f32[32,512,8]{1,2,0:T(8,128)S(1)} async-done(((f32[32,512,8]{1,2,0:T(8,128)}), f32[32,512,8]{1,2,0:T(8,128)S(1)}, u32[]{:S(2)}, u32[]{:S(2)}) %all-to-all-start.2) | async-done | bytes 524320 | tf_op jit(solution)/shard_map/all_to_all | solution.py:31
  91.4 1.3 fusion.2
  92.7 6.3 %all-to-all-start.3 = ((f32[16,256,16]{1,2,0:T(8,128)}), f32[16,256,16]{1,2,0:T(8,128)S(1)}, u32[]{:S(2)}, u32[]{:S(2)}) async-start(f32[16,256,16]{1,2,0:T(8,128)} %bitcast.28), calls=%async_computation.3 | async-start | bytes 524288 | tf_op jit(solution)/shard_map/all_to_all | solution.py:53
  99.0 8.0 %all-to-all-done.3 = f32[16,256,16]{1,2,0:T(8,128)S(1)} async-done(((f32[16,256,16]{1,2,0:T(8,128)}), f32[16,256,16]{1,2,0:T(8,128)S(1)}, u32[]{:S(2)}, u32[]{:S(2)}) %all-to-all-start.3) | async-done | bytes 262176 | tf_op jit(solution)/shard_map/all_to_all | solution.py:53
  107.0 0.1 copy.32
  107.1 0.3 rev.13
  107.6 11.1 %collective-permute-start.2 = (f32[1,16]{0,1:T(8,128)S(1)}, f32[1,16]{0,1:T(8,128)S(1)}, u32[]{:S(2)}, u32[]{:S(2)}) collective-permute-start(f32[1,16]{0,1:T(8,128)S(1)} %get-tuple-element.25), channel_id=1, source_target_pairs={{0,16},{16,32},{32,48},{48,64},{64,80},{80,96},{96,112},{112,128},... | collective-permute-start | bytes 200 | tf_op jit(solution)/shard_map/ppermute | solution.py:20
  118.7 1.9 collective-permute-start.3
  120.6 6.9 %collective-permute-done.3 = f32[1,16]{0,1:T(8,128)S(1)} collective-permute-done((f32[1,16]{0,1:T(8,128)S(1)}, f32[1,16]{0,1:T(8,128)S(1)}, u32[]{:S(2)}, u32[]{:S(2)}) %collective-permute-start.3) | collective-permute-done | bytes 96 | tf_op jit(solution)/shard_map/ppermute | solution.py:22
  127.7 11.3 %all_to_all.40 = f32[16,256,16]{1,2,0:T(8,128)S(1)} all-to-all(f32[16,256,16]{1,2,0:T(8,128)S(1)} %broadcast_in_dim.158), channel_id=1, replica_groups=mesh['cuts'=32,'row'=16] {'row'}, dimensions={0} | all-to-all | bytes 524288 | tf_op jit(solution)/shard_map/all_to_all | solution.py:31
  139.0 1.4 convolution_bitcast_fusion
  140.4 6.8 %all-to-all-start.5 = ((f32[32,512,8]{1,2,0:T(8,128)}), f32[32,512,8]{1,2,0:T(8,128)S(1)}, u32[]{:S(2)}, u32[]{:S(2)}) async-start(f32[32,512,8]{1,2,0:T(8,128)} %convolution_bitcast_fusion), calls=%async_computation.5 | async-start | bytes 1048576 | tf_op jit(solution)/shard_map/all_to_all | solution.py:53
  147.3 18.1 %all-to-all-done.5 = f32[32,512,8]{1,2,0:T(8,128)S(1)} async-done(((f32[32,512,8]{1,2,0:T(8,128)}), f32[32,512,8]{1,2,0:T(8,128)S(1)}, u32[]{:S(2)}, u32[]{:S(2)}) %all-to-all-start.5) | async-done | bytes 524320 | tf_op jit(solution)/shard_map/all_to_all | solution.py:53
  165.5 0.1 copy.34
  165.6 0.6 rev.14
  166.3 0.1 copy.35
  166.5 3.9 %collective-permute-start.4 = (f32[1,8]{0,1:T(8,128)S(1)}, f32[1,8]{0,1:T(8,128)S(1)}, u32[]{:S(2)}, u32[]{:S(2)}) collective-permute-start(f32[1,8]{0,1:T(8,128)S(1)} %get-tuple-element.23), channel_id=1, source_target_pairs={{0,1},{1,2},{2,3},{3,4},{4,5},{5,6},{6,7},{7,8},{8,9},{9,10},{10,1... | collective-permute-start | bytes 104 | tf_op jit(solution)/shard_map/ppermute | solution.py:20
  170.4 5.2 %collective-permute-start.5 = (f32[1,8]{0,1:T(8,128)S(1)}, f32[1,8]{0,1:T(8,128)S(1)}, u32[]{:S(2)}, u32[]{:S(2)}) collective-permute-start(f32[1,8]{0,1:T(8,128)S(1)} %get-tuple-element.24), channel_id=1, source_target_pairs={{1,0},{2,1},{3,2},{4,3},{5,4},{6,5},{7,6},{8,7},{9,8},{10,9},{11,1... | collective-permute-start | bytes 104 | tf_op jit(solution)/shard_map/ppermute | solution.py:22
  175.7 0.7 collective-permute-done.5
  176.5 24.6 %all_to_all.41 = f32[32,512,8]{1,2,0:T(8,128)S(1)} all-to-all(f32[32,512,8]{1,2,0:T(8,128)S(1)} %broadcast_in_dim.159), channel_id=1, replica_groups=mesh['cuts'=32,'row'=16] {'cuts'}, dimensions={0} | all-to-all | bytes 1048576 | tf_op jit(solution)/shard_map/all_to_all | solution.py:31
  201.1 1.3 fusion
  202.4 6.5 %all-to-all-start.7 = ((f32[16,256,16]{1,2,0:T(8,128)}), f32[16,256,16]{1,2,0:T(8,128)S(1)}, u32[]{:S(2)}, u32[]{:S(2)}) async-start(f32[16,256,16]{1,2,0:T(8,128)} %bitcast.42), calls=%async_computation.7 | async-start | bytes 524288 | tf_op jit(solution)/shard_map/all_to_all | solution.py:53
  209.0 8.0 %all-to-all-done.7 = f32[16,256,16]{1,2,0:T(8,128)S(1)} async-done(((f32[16,256,16]{1,2,0:T(8,128)}), f32[16,256,16]{1,2,0:T(8,128)S(1)}, u32[]{:S(2)}, u32[]{:S(2)}) %all-to-all-start.7) | async-done | bytes 262176 | tf_op jit(solution)/shard_map/all_to_all | solution.py:53
  217.0 0.1 copy.36
  217.1 0.3 rev.15
  217.5 11.1 %collective-permute-start.6 = (f32[1,16]{0,1:T(8,128)S(1)}, f32[1,16]{0,1:T(8,128)S(1)}, u32[]{:S(2)}, u32[]{:S(2)}) collective-permute-start(f32[1,16]{0,1:T(8,128)S(1)} %get-tuple-element.21), channel_id=1, source_target_pairs={{0,16},{16,32},{32,48},{48,64},{64,80},{80,96},{96,112},{112,128},... | collective-permute-start | bytes 200 | tf_op jit(solution)/shard_map/ppermute | solution.py:20
  228.6 1.9 collective-permute-start.7
  230.5 6.9 %collective-permute-done.7 = f32[1,16]{0,1:T(8,128)S(1)} collective-permute-done((f32[1,16]{0,1:T(8,128)S(1)}, f32[1,16]{0,1:T(8,128)S(1)}, u32[]{:S(2)}, u32[]{:S(2)}) %collective-permute-start.7) | collective-permute-done | bytes 96 | tf_op jit(solution)/shard_map/ppermute | solution.py:22
  237.5 0.7 fusion.9
  (51 shorter events, 1.6 us)
Async XLA Ops:
  0.0 17.6 %copy-start = (f32[512,256]{1,0:T(8,128)S(1)}, f32[512,256]{1,0:T(8,128)}, u32[]{:S(2)}) copy-start(f32[512,256]{1,0:T(8,128)} %param.5) | copy-start | bytes 1572868
  1.5 8.1 %copy-start.1 = (s32[4,8192]{1,0:T(4,128)S(1)}, s32[4,8192]{1,0:T(4,128)}, u32[]{:S(2)}) copy-start(s32[4,8192]{1,0:T(4,128)} %param.7) | copy-start | bytes 393220
  1.5 16.1 %all-to-all-start = ((f32[16,256,16]{1,2,0:T(8,128)}), f32[16,256,16]{1,2,0:T(8,128)S(1)}, u32[]{:S(2)}, u32[]{:S(2)}) async-start(f32[16,256,16]{1,2,0:T(8,128)} %broadcast_in_dim.154), calls=%async_computation | async-start | bytes 524288 | tf_op jit(solution)/shard_map/all_to_all | solution.py:31
  9.6 0.9 copy-start.2
  19.4 34.6 %all-to-all-start.1 = ((f32[32,512,8]{1,2,0:T(8,128)}), f32[32,512,8]{1,2,0:T(8,128)S(1)}, u32[]{:S(2)}, u32[]{:S(2)}) async-start(f32[32,512,8]{1,2,0:T(8,128)} %copy.28), calls=%async_computation.1 | async-start | bytes 1048576 | tf_op jit(solution)/shard_map/all_to_all | solution.py:53
  39.2 0.7 copy-start.3
  55.0 9.2 %collective-permute-start = (f32[1,8]{0,1:T(8,128)S(1)}, f32[1,8]{0,1:T(8,128)S(1)}, u32[]{:S(2)}, u32[]{:S(2)}) collective-permute-start(f32[1,8]{0,1:T(8,128)S(1)} %get-tuple-element.27), channel_id=1, source_target_pairs={{0,1},{1,2},{2,3},{3,4},{4,5},{5,6},{6,7},{7,8},{8,9},{9,10},{10,1... | collective-permute-start | bytes 104 | tf_op jit(solution)/shard_map/ppermute | solution.py:20
  59.6 5.3 %collective-permute-start.1 = (f32[1,8]{0,1:T(8,128)S(1)}, f32[1,8]{0,1:T(8,128)S(1)}, u32[]{:S(2)}, u32[]{:S(2)}) collective-permute-start(f32[1,8]{0,1:T(8,128)S(1)} %get-tuple-element.28), channel_id=1, source_target_pairs={{1,0},{2,1},{3,2},{4,3},{5,4},{6,5},{7,6},{8,7},{9,8},{10,9},{11,1... | collective-permute-start | bytes 104 | tf_op jit(solution)/shard_map/ppermute | solution.py:22
  65.9 25.5 %all-to-all-start.2 = ((f32[32,512,8]{1,2,0:T(8,128)}), f32[32,512,8]{1,2,0:T(8,128)S(1)}, u32[]{:S(2)}, u32[]{:S(2)}) async-start(f32[32,512,8]{1,2,0:T(8,128)} %broadcast_in_dim.156), calls=%async_computation.2 | async-start | bytes 1048576 | tf_op jit(solution)/shard_map/all_to_all | solution.py:31
  92.7 14.3 %all-to-all-start.3 = ((f32[16,256,16]{1,2,0:T(8,128)}), f32[16,256,16]{1,2,0:T(8,128)S(1)}, u32[]{:S(2)}, u32[]{:S(2)}) async-start(f32[16,256,16]{1,2,0:T(8,128)} %bitcast.28), calls=%async_computation.3 | async-start | bytes 524288 | tf_op jit(solution)/shard_map/all_to_all | solution.py:53
  107.6 13.0 %collective-permute-start.2 = (f32[1,16]{0,1:T(8,128)S(1)}, f32[1,16]{0,1:T(8,128)S(1)}, u32[]{:S(2)}, u32[]{:S(2)}) collective-permute-start(f32[1,16]{0,1:T(8,128)S(1)} %get-tuple-element.25), channel_id=1, source_target_pairs={{0,16},{16,32},{32,48},{48,64},{64,80},{80,96},{96,112},{112,128},... | collective-permute-start | bytes 200 | tf_op jit(solution)/shard_map/ppermute | solution.py:20
  118.7 8.9 %collective-permute-start.3 = (f32[1,16]{0,1:T(8,128)S(1)}, f32[1,16]{0,1:T(8,128)S(1)}, u32[]{:S(2)}, u32[]{:S(2)}) collective-permute-start(f32[1,16]{0,1:T(8,128)S(1)} %get-tuple-element.26), channel_id=1, source_target_pairs={{16,0},{32,16},{48,32},{64,48},{80,64},{96,80},{112,96},{128,112},... | collective-permute-start | bytes 200 | tf_op jit(solution)/shard_map/ppermute | solution.py:22
  140.4 25.0 %all-to-all-start.5 = ((f32[32,512,8]{1,2,0:T(8,128)}), f32[32,512,8]{1,2,0:T(8,128)S(1)}, u32[]{:S(2)}, u32[]{:S(2)}) async-start(f32[32,512,8]{1,2,0:T(8,128)} %convolution_bitcast_fusion), calls=%async_computation.5 | async-start | bytes 1048576 | tf_op jit(solution)/shard_map/all_to_all | solution.py:53
  166.5 9.2 %collective-permute-start.4 = (f32[1,8]{0,1:T(8,128)S(1)}, f32[1,8]{0,1:T(8,128)S(1)}, u32[]{:S(2)}, u32[]{:S(2)}) collective-permute-start(f32[1,8]{0,1:T(8,128)S(1)} %get-tuple-element.23), channel_id=1, source_target_pairs={{0,1},{1,2},{2,3},{3,4},{4,5},{5,6},{6,7},{7,8},{8,9},{9,10},{10,1... | collective-permute-start | bytes 104 | tf_op jit(solution)/shard_map/ppermute | solution.py:20
  170.4 6.0 %collective-permute-start.5 = (f32[1,8]{0,1:T(8,128)S(1)}, f32[1,8]{0,1:T(8,128)S(1)}, u32[]{:S(2)}, u32[]{:S(2)}) collective-permute-start(f32[1,8]{0,1:T(8,128)S(1)} %get-tuple-element.24), channel_id=1, source_target_pairs={{1,0},{2,1},{3,2},{4,3},{5,4},{6,5},{7,6},{8,7},{9,8},{10,9},{11,1... | collective-permute-start | bytes 104 | tf_op jit(solution)/shard_map/ppermute | solution.py:22
  202.4 14.5 %all-to-all-start.7 = ((f32[16,256,16]{1,2,0:T(8,128)}), f32[16,256,16]{1,2,0:T(8,128)S(1)}, u32[]{:S(2)}, u32[]{:S(2)}) async-start(f32[16,256,16]{1,2,0:T(8,128)} %bitcast.42), calls=%async_computation.7 | async-start | bytes 524288 | tf_op jit(solution)/shard_map/all_to_all | solution.py:53
  217.5 13.0 %collective-permute-start.6 = (f32[1,16]{0,1:T(8,128)S(1)}, f32[1,16]{0,1:T(8,128)S(1)}, u32[]{:S(2)}, u32[]{:S(2)}) collective-permute-start(f32[1,16]{0,1:T(8,128)S(1)} %get-tuple-element.21), channel_id=1, source_target_pairs={{0,16},{16,32},{32,48},{48,64},{64,80},{80,96},{96,112},{112,128},... | collective-permute-start | bytes 200 | tf_op jit(solution)/shard_map/ppermute | solution.py:20
  228.6 8.9 %collective-permute-start.7 = (f32[1,16]{0,1:T(8,128)S(1)}, f32[1,16]{0,1:T(8,128)S(1)}, u32[]{:S(2)}, u32[]{:S(2)}) collective-permute-start(f32[1,16]{0,1:T(8,128)S(1)} %get-tuple-element.22), channel_id=1, source_target_pairs={{16,0},{32,16},{48,32},{64,48},{80,64},{96,80},{112,96},{128,112},... | collective-permute-start | bytes 200 | tf_op jit(solution)/shard_map/ppermute | solution.py:22
where the time goes:
time: 239 us; the launch traced here: 238 us
  starting transfers between devices  97.5 us (41%)
  waiting for transfers between devices  84.7 us (35%)
  blocking collectives  35.9 us (15%)
  local copies, waits for them, and re-layouts  10.7 us (4%)
  matrix products  4.7 us (2%)
  other arithmetic  4.29 us (2%)
    all_to_all x4, waiting for transfers between devices, sent_and_summed(): lax.all_to_all(parts, axis, split_axis=0, concat_axis=0, tiled=True)  48 us
    all_to_all x4, starting transfers between devices, sent_and_summed(): lax.all_to_all(parts, axis, split_axis=0, concat_axis=0, tiled=True)  36.5 us
    all_to_all x2, blocking collectives, from_everyone(): lax.all_to_all(jnp.broadcast_to(x[None], (peers, *x.shape)), axis, 0, 0,...  35.9 us
    ppermute x4, starting transfers between devices, extended(): lax.ppermute(tail, axis, [(i, (i + 1) % count) for i in range(count)])  30.7 us
    all_to_all x2, waiting for transfers between devices, from_everyone(): lax.all_to_all(jnp.broadcast_to(x[None], (peers, *x.shape)), axis, 0, 0,...  21.4 us
    all_to_all x2, starting transfers between devices, from_everyone(): lax.all_to_all(jnp.broadcast_to(x[None], (peers, *x.shape)), axis, 0, 0,...  16.6 us
    ppermute x4, waiting for transfers between devices, extended(): lax.ppermute(head, axis, [((i + 1) % count, i) for i in range(count)])  15.3 us
    ppermute x4, starting transfers between devices, extended(): lax.ppermute(head, axis, [((i + 1) % count, i) for i in range(count)])  13.7 us
  transfers between devices with their start and end apart: 14, of which 10 were waited for; matrix products, arithmetic and copies ran while one was open for 3% of the time, Pallas kernels for 0%

commit v1 on v0

v1 whole, which is shorter than its diff:
```python
import functools

import jax
import jax.numpy as jnp
from jax import lax
from jax.experimental import pallas as pl
from jax.experimental.pallas import tpu as pltpu
from jax.sharding import Mesh, PartitionSpec as P

SITES = 8192
SLICES = 4

hs_strength = 0.3

ROW = ("x", "ylo")
CUT = ("z", "yhi")


def twin(x):
    return lax.ppermute(x, "core", [(0, 1), (1, 0)])


def shifted(x, axes, step):
    count = lax.axis_size(axes)
    return lax.ppermute(x, axes, [(i, (i + step) % count) for i in range(count)])


def exchanged(parts, axes):
    return lax.all_to_all(parts, axes, 0, 0, tiled=True)


def gathered(x, axes):
    count = lax.axis_size(axes)
    parts = exchanged(jnp.broadcast_to(x[None], (count, *x.shape)), axes)
    return parts.reshape(count * x.shape[0], x.shape[1])


def summed(x, axes):
    count = lax.axis_size(axes)
    return exchanged(x.reshape(count, x.shape[0] // count, x.shape[1]), axes).sum(axis=0)


def lookup(indices, couplings):
    levels = jnp.arange(couplings.shape[0], dtype=jnp.int32)
    hits = indices[None, :] == levels[:, None]
    return jnp.sum(jnp.where(hits, couplings[:, None], 0.0), axis=0)


def mixing(slice_no, first, count, fields, phonon, couplings):
    levels = phonon[slice_no]
    window = lax.dynamic_slice_in_dim(levels, first, count)
    before = lax.dynamic_slice_in_dim(levels, (first - 2 + SITES) % SITES, 2)
    after = lax.dynamic_slice_in_dim(levels, (first + count) % SITES, 2)
    rate = lookup(window, couplings)
    edge = lookup(jnp.concatenate([before, after]), couplings)
    even = jnp.arange(count, dtype=jnp.int32) % 2 == 0
    left = jnp.concatenate([edge[1:2], rate[:-1]])
    even_rate = jnp.where(even, rate, left)
    odd_rate = jnp.where(even, left, rate)
    signs = (2 * lax.dynamic_slice_in_dim(fields[slice_no], first, count) - 1).astype(jnp.float32)
    scale = jnp.exp(hs_strength * signs)
    outer = jnp.concatenate([edge[0:1], edge[2:3]])
    outer = jnp.concatenate([jnp.cosh(outer), jnp.sinh(outer)])
    outer = jnp.pad(outer, (0, count - 4))
    zero = jnp.zeros_like(rate)
    return jnp.stack(
        [
            jnp.cosh(even_rate),
            jnp.sinh(even_rate),
            scale * jnp.cosh(odd_rate),
            scale * jnp.sinh(odd_rate),
            outer,
            zero,
            zero,
            zero,
        ]
    )


def halves(x):
    high = x.astype(jnp.bfloat16)
    return high, (x - high.astype(jnp.float32)).astype(jnp.bfloat16)


def product(a, b, contract_b):
    dims = (((1,), (contract_b,)), ((), ()))
    dot = functools.partial(lax.dot_general, dimension_numbers=dims, preferred_element_type=jnp.float32)
    a_high, a_low = halves(a)
    b_high, b_low = halves(b)
    return dot(a_high, b_high) + (dot(a_high, b_low) + dot(a_low, b_high))


def slice_kernel(across, core_ref, u_ref, mine_ref, other_ref, rim_ref, mix_ref, out_ref, w_ref):
    width = mine_ref.shape[1]
    core = core_ref[0]
    at_mine = pl.ds(pl.multiple_of(core * width, width), width)
    at_other = pl.ds(pl.multiple_of((1 - core) * width, width), width)
    mix = mix_ref[...]
    rim = rim_ref[...]
    rim_left = mix[4:5, 2:3] * rim[0:1] + mix[4:5, 0:1] * rim[1:2]
    rim_right = mix[4:5, 1:2] * rim[2:3] + mix[4:5, 3:4] * rim[3:4]
    if across:
        u_mine, u_other = u_ref[:, at_mine], u_ref[:, at_other]
        w = product(u_mine, mine_ref[...], 1) + product(u_other, other_ref[...], 1)
        u = jnp.concatenate([u_mine, u_other], axis=1)
    else:
        u = u_ref[...]
        w_ref[:, at_mine] = product(u, mine_ref[...], 0)
        w_ref[:, at_other] = product(u, other_ref[...], 0)
        w = w_ref[...]
    end_left = jnp.sum(u * rim_left, axis=1, keepdims=True)
    end_right = jnp.sum(u * rim_right, axis=1, keepdims=True)
    count = w.shape[1]
    lane = lax.broadcasted_iota(jnp.int32, w.shape, 1)
    even = lane % 2 == 0
    partner = jnp.where(even, pltpu.roll(w, count - 1, 1), pltpu.roll(w, 1, 1))
    e = mix[0:1] * w + mix[1:2] * partner
    below = jnp.where(lane == 0, end_left, pltpu.roll(e, 1, 1))
    above = jnp.where(lane == count - 1, end_right, pltpu.roll(e, count - 1, 1))
    out_ref[...] = mix[2:3] * e + mix[3:4] * jnp.where(even, below, above)


def one_slice(across, core, u, mine, other, rim, mix):
    columns, depth = u.shape
    sites = mine.shape[0] if across else 2 * mine.shape[1]
    vmem = pl.BlockSpec(memory_space=pltpu.VMEM)
    return pl.pallas_call(
        functools.partial(slice_kernel, across),
        out_shape=jax.ShapeDtypeStruct((columns, sites), jnp.float32),
        in_specs=[pl.BlockSpec(memory_space=pltpu.SMEM)] + [vmem] * 5,
        out_specs=vmem,
        scratch_shapes=[pltpu.VMEM((columns, sites), jnp.float32)],
        compiler_params=pltpu.CompilerParams(vmem_limit_bytes=24 * 1024 * 1024),
        cost_estimate=pl.CostEstimate(
            flops=12 * columns * depth * sites, bytes_accessed=8 * depth * sites, transcendentals=0
        ),
        name="across" if across else "along",
    )(core, u, mine, other, rim, mix)


def shards(propagator, slab, fields, phonon, couplings):
    core = lax.axis_index("core")
    first_core = core == 0
    columns = slab.T
    half = columns.shape[0] // 2
    near = columns.shape[1]

    kept = lax.dynamic_slice_in_dim(columns, core * half, half, axis=0)
    given = lax.dynamic_slice_in_dim(columns, (1 - core) * half, half, axis=0)
    taken = twin(given)
    both = jnp.where(first_core, jnp.concatenate([kept, taken], 1), jnp.concatenate([taken, kept], 1))
    u = gathered(both, ROW)

    mine = propagator
    other = twin(propagator)
    block = mine.shape[0]
    count = 2 * mine.shape[1]

    def rims(low, high, axes):
        before = shifted(high, axes, 1)
        after = shifted(low, axes, -1)
        return jnp.concatenate([before, after, jnp.zeros((4, before.shape[1]), jnp.float32)], axis=0)

    row_rim = rims(
        jnp.concatenate([mine[:2], other[:2]], axis=1),
        jnp.concatenate([mine[-2:], other[-2:]], axis=1),
        ROW,
    )
    first = jnp.where(first_core, mine[:, :2], other[:, :2]).T
    last = jnp.where(first_core, other[:, -2:], mine[:, -2:]).T
    cut_rim = rims(first, last, CUT)

    row_first = lax.axis_index(ROW) * block
    cut_first = lax.axis_index(CUT) * count
    which = jnp.reshape(core, (1,)).astype(jnp.int32)
    for slice_no in range(SLICES):
        across = slice_no % 2 == 0
        if across:
            mix = mixing(slice_no, row_first, block, fields, phonon, couplings)
        else:
            mix = mixing(slice_no, cut_first, count, fields, phonon, couplings)
        w = one_slice(across, which, u, mine, other, row_rim if across else cut_rim, mix)
        axes = CUT if across else ROW
        share = summed(w, axes)
        if slice_no < SLICES - 1:
            u = gathered(share, axes)
    kept = lax.dynamic_slice_in_dim(share, core * near, near, axis=1)
    given = lax.dynamic_slice_in_dim(share, (1 - core) * near, near, axis=1)
    taken = twin(given)
    out = jnp.where(first_core, jnp.concatenate([kept, taken], 0), jnp.concatenate([taken, kept], 0))
    return out.T


def solution(mesh):
    devices = mesh.devices.reshape(8, 2, 2, 4, 4)
    fine = Mesh(devices, ("z", "yhi", "core", "x", "ylo"))
    cuts, row = ("z", "yhi", "core"), ROW
    in_specs = (P(row, cuts), P(cuts, row), P(), P(), P())
    return jax.shard_map(shards, mesh=fine, in_specs=in_specs, out_specs=P(cuts, row), check_vma=False)
```

time: 239 us -> 195 us (0.82)
  blocking collectives: 35.9 us -> 0 us
  starting transfers between devices: 97.5 us -> 81.6 us
  other arithmetic: 4.29 us -> 15.8 us
  Pallas kernels: 0 us -> 6.39 us
  waiting for transfers between devices: 84.7 us -> 78.9 us
  matrix products: 4.7 us -> 0 us
    all_to_all x2 -> x0, blocking collectives: 35.9 us -> none  [from_everyone(): lax.all_to_all(jnp.broadcast_to(x[None], (peers, *x.shape)), axis, 0, 0,...]
    all_to_all x6 -> x8, starting transfers between devices: 53.1 us -> 42.9 us  [exchanged(): return lax.all_to_all(parts, axes, 0, 0, tiled=True)]
    pallas_call x0 -> x4, Pallas kernels: none -> 6.39 us  [one_slice(): pl.pallas_call(functools.partial(slice_kernel, across), out_shape=jax.Sha...]
    ppermute x8 -> x7, starting transfers between devices: 44.4 us -> 38.7 us  [the longest x4 22.5 us: shifted(): lax.ppermute(x, axes, [(i, (i + step) % count) for i in range(count)])]
    sinh x0 -> x4, other arithmetic: none -> 5.49 us  [mixing(): outer = jnp.concatenate([jnp.cosh(outer), jnp.sinh(outer)])]
    all_to_all x6 -> x8, waiting for transfers between devices: 69.3 us -> 63.9 us  [exchanged(): return lax.all_to_all(parts, axes, 0, 0, tiled=True)]
    cosh x8 -> x4, other arithmetic: 0.14 us -> 5.49 us  [mixing(): outer = jnp.concatenate([jnp.cosh(outer), jnp.sinh(outer)])]
    dot_general x4 -> x0, matrix products: 4.7 us -> none  [the longest x2 2.61 us: shards(): lax.dot_general(propagator, gather_directly(current, 'cuts', 1), (((0,),...]
  transfers between devices with their start and end apart: 14 -> 15, of which waited for: 10 -> 10; matrix products, arithmetic and copies ran while one was open for 3% -> 11% of each run, Pallas kernels for 0% -> 0%
where the time goes in v1:
time: 195 us; the launch traced here: 193 us
  starting transfers between devices  81.6 us (42%)
  waiting for transfers between devices  78.9 us (40%)
  other arithmetic  15.8 us (8%)
  local copies, waits for them, and re-layouts  10 us (5%)
  Pallas kernels  6.39 us (3%)
    all_to_all x8, waiting for transfers between devices, exchanged(): return lax.all_to_all(parts, axes, 0, 0, tiled=True)  63.9 us
    all_to_all x8, starting transfers between devices, exchanged(): return lax.all_to_all(parts, axes, 0, 0, tiled=True)  42.9 us
    ppermute x4, starting transfers between devices, shifted(): lax.ppermute(x, axes, [(i, (i + step) % count) for i in range(count)])  22.5 us
    ppermute x3, starting transfers between devices, twin(): return lax.ppermute(x, 'core', [(0, 1), (1, 0)])  16.1 us
    ppermute x4, waiting for transfers between devices, shifted(): lax.ppermute(x, axes, [(i, (i + step) % count) for i in range(count)])  14.2 us
    pallas_call x4, Pallas kernels, one_slice(): pl.pallas_call(functools.partial(slice_kernel, across), out_shape=jax.Sha...  6.39 us
    sinh x4, other arithmetic, mixing(): outer = jnp.concatenate([jnp.cosh(outer), jnp.sinh(outer)])  5.49 us
    cosh x4, other arithmetic, mixing(): outer = jnp.concatenate([jnp.cosh(outer), jnp.sinh(outer)])  5.49 us
  transfers between devices with their start and end apart: 15, of which 10 were waited for; matrix products, arithmetic and copies ran while one was open for 11% of the time, Pallas kernels for 0%

profile of v1, /device:TPU:1, one launch (start us, length us, event | category | flops | bytes accessed | tf_op | source)
XLA Modules:
  0.0 193.0 jit_solution(9819240592419160424)
XLA Ops:
  0.0 0.7 copy-done.1
  0.7 8.7 %collective-permute-start = (f32[8,256]{1,0:T(8,128)S(1)}, f32[8,256]{1,0:T(8,128)S(1)}, u32[]{:S(2)}, u32[]{:S(2)}) collective-permute-start(f32[8,256]{1,0:T(8,128)S(1)} %get-tuple-element.46), channel_id=1, source_target_pairs={{0,16},{16,0},{1,17},{17,1},{2,18},{18,2},{3,19},{19,3},{4,20},{20... | collective-permute-start | bytes 24584 | tf_op jit(solution)/shard_map/ppermute | solution.py:20
  9.5 1.9 collective-permute-start.1
  11.5 1.4 fusion.55
  12.9 0.1 fusion.44
  13.0 0.1 fusion.40
  13.1 1.3 fusion.54
  14.6 0.6 copy-done.2
  15.2 0.2 select_reduce_fusion.4
  15.4 0.6 fusion.59
  16.0 0.1 select_reduce_fusion
  16.2 0.7 fusion.20
  16.9 1.3 compare_select_fusion.11
  18.2 1.3 fusion.48
  19.5 0.7 broadcast_in_dim.96
  20.2 3.5 %all-to-all-start = ((f32[16,8,512]{2,1,0:T(8,128)}), f32[16,8,512]{2,1,0:T(8,128)S(1)}, u32[]{:S(2)}, u32[]{:S(2)}) async-start(f32[16,8,512]{2,1,0:T(8,128)} %broadcast_in_dim.96), calls=%async_computation | async-start | bytes 524288 | tf_op jit(solution)/shard_map/all_to_all | solution.py:29
  23.8 0.2 fusion.1
  24.0 11.5 %collective-permute-start.5 = (f32[2,512]{0,1:T(8,128)S(1)}, f32[2,512]{0,1:T(8,128)S(1)}, u32[]{:S(2)}, u32[]{:S(2)}) collective-permute-start(f32[2,512]{0,1:T(8,128)S(1)} %get-tuple-element.14), channel_id=1, source_target_pairs={{0,480},{32,0},{64,32},{96,64},{128,96},{160,128},{192,160},{224,1... | collective-permute-start | bytes 12296 | tf_op jit(solution)/shard_map/ppermute | solution.py:25
  35.5 1.9 collective-permute-start.4
  37.5 7.2 %collective-permute-start.3 = (f32[2,512]{1,0:T(2,128)S(1)}, f32[2,512]{1,0:T(2,128)S(1)}, u32[]{:S(2)}, u32[]{:S(2)}) collective-permute-start(f32[2,512]{1,0:T(2,128)S(1)} %pad_maximum_fusion.1), channel_id=1, source_target_pairs={{0,15},{1,0},{2,1},{3,2},{4,3},{5,4},{6,5},{7,6},{8,7},{9,8},{10,9... | collective-permute-start | bytes 12296 | tf_op jit(solution)/shard_map/ppermute | solution.py:25
  44.7 1.9 collective-permute-start.2
  46.8 0.1 copy.9
  46.9 10.3 %collective-permute-done.4 = f32[2,512]{0,1:T(8,128)S(1)} collective-permute-done((f32[2,512]{0,1:T(8,128)S(1)}, f32[2,512]{0,1:T(8,128)S(1)}, u32[]{:S(2)}, u32[]{:S(2)}) %collective-permute-start.4) | collective-permute-done | bytes 4128 | tf_op jit(solution)/shard_map/ppermute | solution.py:25
  57.2 0.1 copy.8
  57.3 3.9 %collective-permute-done.2 = f32[2,512]{1,0:T(2,128)S(1)} collective-permute-done((f32[2,512]{1,0:T(2,128)S(1)}, f32[2,512]{1,0:T(2,128)S(1)}, u32[]{:S(2)}, u32[]{:S(2)}) %collective-permute-start.2) | collective-permute-done | bytes 4128 | tf_op jit(solution)/shard_map/ppermute | solution.py:25
  61.3 1.7 across.2
  63.0 3.6 %all-to-all-start.1 = ((f32[16,8,512]{2,1,0:T(8,128)}), f32[16,8,512]{2,1,0:T(8,128)S(1)}, u32[]{:S(2)}, u32[]{:S(2)}) async-start(f32[16,8,512]{2,1,0:T(8,128)} %bitcast.11), calls=%async_computation.1 | async-start | bytes 524288 | tf_op jit(solution)/shard_map/all_to_all | solution.py:29
  66.6 0.6 fusion.58
  67.2 11.8 %all-to-all-done.1 = f32[16,8,512]{2,1,0:T(8,128)S(1)} async-done(((f32[16,8,512]{2,1,0:T(8,128)}), f32[16,8,512]{2,1,0:T(8,128)S(1)}, u32[]{:S(2)}, u32[]{:S(2)}) %all-to-all-start.1) | async-done | bytes 262176 | tf_op jit(solution)/shard_map/all_to_all | solution.py:29
  79.0 0.7 broadcast_in_dim.101
  79.8 5.8 %all-to-all-start.2 = ((f32[16,8,512]{2,1,0:T(8,128)}), f32[16,8,512]{2,1,0:T(8,128)S(1)}, u32[]{:S(2)}, u32[]{:S(2)}) async-start(f32[16,8,512]{2,1,0:T(8,128)} %broadcast_in_dim.101), calls=%async_computation.2 | async-start | bytes 524288 | tf_op jit(solution)/shard_map/all_to_all | solution.py:29
  85.6 1.4 compare_select_fusion.10
  87.0 1.4 fusion.49
  88.4 0.1 select_maximum_fusion.2
  88.5 0.7 fusion.21
  89.3 8.9 %all-to-all-done.2 = f32[16,8,512]{2,1,0:T(8,128)S(1)} async-done(((f32[16,8,512]{2,1,0:T(8,128)}), f32[16,8,512]{2,1,0:T(8,128)S(1)}, u32[]{:S(2)}, u32[]{:S(2)}) %all-to-all-start.2) | async-done | bytes 262176 | tf_op jit(solution)/shard_map/all_to_all | solution.py:29
  98.2 1.5 along.2
  99.7 10.1 %all-to-all-start.3 = ((f32[16,8,512]{2,1,0:T(8,128)}), f32[16,8,512]{2,1,0:T(8,128)S(1)}, u32[]{:S(2)}, u32[]{:S(2)}) async-start(f32[16,8,512]{2,1,0:T(8,128)} %bitcast.22), calls=%async_computation.3 | async-start | bytes 524288 | tf_op jit(solution)/shard_map/all_to_all | solution.py:29
  109.8 0.6 fusion.57
  110.4 9.1 %all-to-all-done.3 = f32[16,8,512]{2,1,0:T(8,128)S(1)} async-done(((f32[16,8,512]{2,1,0:T(8,128)}), f32[16,8,512]{2,1,0:T(8,128)S(1)}, u32[]{:S(2)}, u32[]{:S(2)}) %all-to-all-start.3) | async-done | bytes 262176 | tf_op jit(solution)/shard_map/all_to_all | solution.py:29
  119.6 0.7 broadcast_in_dim.102
  120.3 3.9 %all-to-all-start.4 = ((f32[16,8,512]{2,1,0:T(8,128)}), f32[16,8,512]{2,1,0:T(8,128)S(1)}, u32[]{:S(2)}, u32[]{:S(2)}) async-start(f32[16,8,512]{2,1,0:T(8,128)} %broadcast_in_dim.102), calls=%async_computation.4 | async-start | bytes 524288 | tf_op jit(solution)/shard_map/all_to_all | solution.py:29
  124.2 1.4 compare_select_fusion.9
  125.6 1.4 fusion.50
  127.0 0.1 select_maximum_fusion.1
  127.1 0.7 fusion.22
  127.9 5.0 %all-to-all-done.4 = f32[16,8,512]{2,1,0:T(8,128)S(1)} async-done(((f32[16,8,512]{2,1,0:T(8,128)}), f32[16,8,512]{2,1,0:T(8,128)S(1)}, u32[]{:S(2)}, u32[]{:S(2)}) %all-to-all-start.4) | async-done | bytes 262176 | tf_op jit(solution)/shard_map/all_to_all | solution.py:29
  132.8 1.7 across.3
  134.5 4.1 %all-to-all-start.5 = ((f32[16,8,512]{2,1,0:T(8,128)}), f32[16,8,512]{2,1,0:T(8,128)S(1)}, u32[]{:S(2)}, u32[]{:S(2)}) async-start(f32[16,8,512]{2,1,0:T(8,128)} %bitcast.31), calls=%async_computation.5 | async-start | bytes 524288 | tf_op jit(solution)/shard_map/all_to_all | solution.py:29
  138.6 0.6 fusion.56
  139.2 11.9 %all-to-all-done.5 = f32[16,8,512]{2,1,0:T(8,128)S(1)} async-done(((f32[16,8,512]{2,1,0:T(8,128)}), f32[16,8,512]{2,1,0:T(8,128)S(1)}, u32[]{:S(2)}, u32[]{:S(2)}) %all-to-all-start.5) | async-done | bytes 262176 | tf_op jit(solution)/shard_map/all_to_all | solution.py:29
  151.2 0.7 broadcast_in_dim.103
  151.9 3.5 %all-to-all-start.6 = ((f32[16,8,512]{2,1,0:T(8,128)}), f32[16,8,512]{2,1,0:T(8,128)S(1)}, u32[]{:S(2)}, u32[]{:S(2)}) async-start(f32[16,8,512]{2,1,0:T(8,128)} %broadcast_in_dim.103), calls=%async_computation.6 | async-start | bytes 524288 | tf_op jit(solution)/shard_map/all_to_all | solution.py:29
  155.4 1.4 compare_select_fusion.8
  156.8 1.4 fusion.51
  158.2 0.1 select_maximum_fusion
  158.3 0.7 fusion.23
  159.1 8.9 %all-to-all-done.6 = f32[16,8,512]{2,1,0:T(8,128)S(1)} async-done(((f32[16,8,512]{2,1,0:T(8,128)}), f32[16,8,512]{2,1,0:T(8,128)S(1)}, u32[]{:S(2)}, u32[]{:S(2)}) %all-to-all-start.6) | async-done | bytes 262176 | tf_op jit(solution)/shard_map/all_to_all | solution.py:29
  167.9 1.5 along.3
  169.5 8.3 %all-to-all-start.7 = ((f32[16,8,512]{2,1,0:T(8,128)}), f32[16,8,512]{2,1,0:T(8,128)S(1)}, u32[]{:S(2)}, u32[]{:S(2)}) async-start(f32[16,8,512]{2,1,0:T(8,128)} %bitcast.40), calls=%async_computation.7 | async-start | bytes 524288 | tf_op jit(solution)/shard_map/all_to_all | solution.py:29
  177.8 8.3 %all-to-all-done.7 = f32[16,8,512]{2,1,0:T(8,128)S(1)} async-done(((f32[16,8,512]{2,1,0:T(8,128)}), f32[16,8,512]{2,1,0:T(8,128)S(1)}, u32[]{:S(2)}, u32[]{:S(2)}) %all-to-all-start.7) | async-done | bytes 262176 | tf_op jit(solution)/shard_map/all_to_all | solution.py:29
  186.1 5.5 %collective-permute-start.6 = (f32[8,256]{1,0:T(8,128)S(1)}, f32[8,256]{1,0:T(8,128)S(1)}, u32[]{:S(2)}, u32[]{:S(2)}) collective-permute-start(f32[8,256]{1,0:T(8,128)S(1)} %get-tuple-element.44), channel_id=1, source_target_pairs={{0,16},{16,0},{1,17},{17,1},{2,18},{18,2},{3,19},{19,3},{4,20},{20... | collective-permute-start | bytes 24584 | tf_op jit(solution)/shard_map/ppermute | solution.py:20
  191.6 0.8 collective-permute-done.6
  192.4 0.6 fusion.2
  (36 shorter events, 0.8 us)
Async XLA Ops:
  0.0 0.7 copy-start.1
  0.0 18.2 %copy-start = (f32[512,256]{1,0:T(8,128)S(1)}, f32[512,256]{1,0:T(8,128)}, u32[]{:S(2)}) copy-start(f32[512,256]{1,0:T(8,128)} %mine_ref.7) | copy-start | bytes 1572868
  0.7 18.8 %collective-permute-start = (f32[8,256]{1,0:T(8,128)S(1)}, f32[8,256]{1,0:T(8,128)S(1)}, u32[]{:S(2)}, u32[]{:S(2)}) collective-permute-start(f32[8,256]{1,0:T(8,128)S(1)} %get-tuple-element.46), channel_id=1, source_target_pairs={{0,16},{16,0},{1,17},{17,1},{2,18},{18,2},{3,19},{19,3},{4,20},{20... | collective-permute-start | bytes 24584 | tf_op jit(solution)/shard_map/ppermute | solution.py:20
  9.5 14.3 %collective-permute-start.1 = (f32[512,256]{1,0:T(8,128)}, f32[512,256]{1,0:T(8,128)S(1)}, u32[]{:S(2)}, u32[]{:S(2)}) collective-permute-start(f32[512,256]{1,0:T(8,128)} %mine_ref.7), channel_id=1, source_target_pairs={{0,16},{16,0},{1,17},{17,1},{2,18},{18,2},{3,19},{19,3},{4,20},{20... | collective-permute-start | bytes 1572872 | tf_op jit(solution)/shard_map/ppermute | solution.py:20
  14.5 0.7 copy-start.2
  20.2 41.1 %all-to-all-start = ((f32[16,8,512]{2,1,0:T(8,128)}), f32[16,8,512]{2,1,0:T(8,128)S(1)}, u32[]{:S(2)}, u32[]{:S(2)}) async-start(f32[16,8,512]{2,1,0:T(8,128)} %broadcast_in_dim.96), calls=%async_computation | async-start | bytes 524288 | tf_op jit(solution)/shard_map/all_to_all | solution.py:29
  24.0 22.8 %collective-permute-start.5 = (f32[2,512]{0,1:T(8,128)S(1)}, f32[2,512]{0,1:T(8,128)S(1)}, u32[]{:S(2)}, u32[]{:S(2)}) collective-permute-start(f32[2,512]{0,1:T(8,128)S(1)} %get-tuple-element.14), channel_id=1, source_target_pairs={{0,480},{32,0},{64,32},{96,64},{128,96},{160,128},{192,160},{224,1... | collective-permute-start | bytes 12296 | tf_op jit(solution)/shard_map/ppermute | solution.py:25
  35.5 21.7 %collective-permute-start.4 = (f32[2,512]{0,1:T(8,128)S(1)}, f32[2,512]{0,1:T(8,128)S(1)}, u32[]{:S(2)}, u32[]{:S(2)}) collective-permute-start(f32[2,512]{0,1:T(8,128)S(1)} %get-tuple-element.13), channel_id=1, source_target_pairs={{0,32},{32,64},{64,96},{96,128},{128,160},{160,192},{192,224},{224... | collective-permute-start | bytes 12296 | tf_op jit(solution)/shard_map/ppermute | solution.py:25
  37.5 19.9 %collective-permute-start.3 = (f32[2,512]{1,0:T(2,128)S(1)}, f32[2,512]{1,0:T(2,128)S(1)}, u32[]{:S(2)}, u32[]{:S(2)}) collective-permute-start(f32[2,512]{1,0:T(2,128)S(1)} %pad_maximum_fusion.1), channel_id=1, source_target_pairs={{0,15},{1,0},{2,1},{3,2},{4,3},{5,4},{6,5},{7,6},{8,7},{9,8},{10,9... | collective-permute-start | bytes 12296 | tf_op jit(solution)/shard_map/ppermute | solution.py:25
  44.7 16.6 %collective-permute-start.2 = (f32[2,512]{1,0:T(2,128)S(1)}, f32[2,512]{1,0:T(2,128)S(1)}, u32[]{:S(2)}, u32[]{:S(2)}) collective-permute-start(f32[2,512]{1,0:T(2,128)S(1)} %pad_maximum_fusion), channel_id=1, source_target_pairs={{0,1},{1,2},{2,3},{3,4},{4,5},{5,6},{6,7},{7,8},{8,9},{9,10},{10,1... | collective-permute-start | bytes 12296 | tf_op jit(solution)/shard_map/ppermute | solution.py:25
  63.0 16.1 %all-to-all-start.1 = ((f32[16,8,512]{2,1,0:T(8,128)}), f32[16,8,512]{2,1,0:T(8,128)S(1)}, u32[]{:S(2)}, u32[]{:S(2)}) async-start(f32[16,8,512]{2,1,0:T(8,128)} %bitcast.11), calls=%async_computation.1 | async-start | bytes 524288 | tf_op jit(solution)/shard_map/all_to_all | solution.py:29
  79.8 18.4 %all-to-all-start.2 = ((f32[16,8,512]{2,1,0:T(8,128)}), f32[16,8,512]{2,1,0:T(8,128)S(1)}, u32[]{:S(2)}, u32[]{:S(2)}) async-start(f32[16,8,512]{2,1,0:T(8,128)} %broadcast_in_dim.101), calls=%async_computation.2 | async-start | bytes 524288 | tf_op jit(solution)/shard_map/all_to_all | solution.py:29
  99.7 19.8 %all-to-all-start.3 = ((f32[16,8,512]{2,1,0:T(8,128)}), f32[16,8,512]{2,1,0:T(8,128)S(1)}, u32[]{:S(2)}, u32[]{:S(2)}) async-start(f32[16,8,512]{2,1,0:T(8,128)} %bitcast.22), calls=%async_computation.3 | async-start | bytes 524288 | tf_op jit(solution)/shard_map/all_to_all | solution.py:29
  120.3 12.5 %all-to-all-start.4 = ((f32[16,8,512]{2,1,0:T(8,128)}), f32[16,8,512]{2,1,0:T(8,128)S(1)}, u32[]{:S(2)}, u32[]{:S(2)}) async-start(f32[16,8,512]{2,1,0:T(8,128)} %broadcast_in_dim.102), calls=%async_computation.4 | async-start | bytes 524288 | tf_op jit(solution)/shard_map/all_to_all | solution.py:29
  134.5 16.6 %all-to-all-start.5 = ((f32[16,8,512]{2,1,0:T(8,128)}), f32[16,8,512]{2,1,0:T(8,128)S(1)}, u32[]{:S(2)}, u32[]{:S(2)}) async-start(f32[16,8,512]{2,1,0:T(8,128)} %bitcast.31), calls=%async_computation.5 | async-start | bytes 524288 | tf_op jit(solution)/shard_map/all_to_all | solution.py:29
  151.9 16.1 %all-to-all-start.6 = ((f32[16,8,512]{2,1,0:T(8,128)}), f32[16,8,512]{2,1,0:T(8,128)S(1)}, u32[]{:S(2)}, u32[]{:S(2)}) async-start(f32[16,8,512]{2,1,0:T(8,128)} %broadcast_in_dim.103), calls=%async_computation.6 | async-start | bytes 524288 | tf_op jit(solution)/shard_map/all_to_all | solution.py:29
  169.5 16.6 %all-to-all-start.7 = ((f32[16,8,512]{2,1,0:T(8,128)}), f32[16,8,512]{2,1,0:T(8,128)S(1)}, u32[]{:S(2)}, u32[]{:S(2)}) async-start(f32[16,8,512]{2,1,0:T(8,128)} %bitcast.40), calls=%async_computation.7 | async-start | bytes 524288 | tf_op jit(solution)/shard_map/all_to_all | solution.py:29
  186.1 6.3 %collective-permute-start.6 = (f32[8,256]{1,0:T(8,128)S(1)}, f32[8,256]{1,0:T(8,128)S(1)}, u32[]{:S(2)}, u32[]{:S(2)}) collective-permute-start(f32[8,256]{1,0:T(8,128)S(1)} %get-tuple-element.44), channel_id=1, source_target_pairs={{0,16},{16,0},{1,17},{17,1},{2,18},{18,2},{3,19},{19,3},{4,20},{20... | collective-permute-start | bytes 24584 | tf_op jit(solution)/shard_map/ppermute | solution.py:20

commit v2 on v1

v2 whole, which is shorter than its diff:
```python
import functools

import jax
import jax.numpy as jnp
from jax import lax
from jax.experimental import pallas as pl
from jax.experimental.pallas import tpu as pltpu
from jax.sharding import Mesh, PartitionSpec as P

SITES = 8192
SLICES = 4
LEVELS = 16
LANES = 128

hs_strength = 0.3

ROW = ("x", "ylo")
CUT = ("z", "yhi")
PAIRED_ROW = ("core", "x", "ylo")

VMEM = pl.BlockSpec(memory_space=pltpu.VMEM)
SMEM = pl.BlockSpec(memory_space=pltpu.SMEM)


def swapped(x, axis):
    return lax.ppermute(x, axis, [(0, 1), (1, 0)])


def exchanged(parts, axes):
    return lax.all_to_all(parts, axes, 0, 0, tiled=True)


def gathered(x, axes):
    count = lax.axis_size(axes)
    parts = exchanged(jnp.broadcast_to(x[None], (count, *x.shape)), axes)
    return parts.reshape(count * x.shape[0], x.shape[1])


def summed(x, axes):
    count = lax.axis_size(axes)
    return exchanged(x.reshape(count, x.shape[0] // count, x.shape[1]), axes).sum(axis=0)


def call(kernel, name, out_shape, in_specs, scratch=(), flops=0, size=0):
    return pl.pallas_call(
        kernel,
        out_shape=out_shape,
        in_specs=in_specs,
        out_specs=jax.tree.map(lambda _: VMEM, out_shape),
        scratch_shapes=list(scratch),
        compiler_params=pltpu.CompilerParams(vmem_limit_bytes=24 * 1024 * 1024),
        cost_estimate=pl.CostEstimate(flops=flops, bytes_accessed=size, transcendentals=0),
        name=name,
    )


def mixing_kernel(first_ref, couplings_ref, phonon_ref, fields_ref, out_ref):
    count = out_ref.shape[2]
    for turn in range(2):
        first = first_ref[turn]
        at_before = pl.ds(pl.multiple_of((first + (SITES - LANES)) % SITES, LANES), LANES)
        at_block = pl.ds(pl.multiple_of(first, LANES), count)
        at_after = pl.ds(pl.multiple_of((first + count) % SITES, LANES), LANES)
        level = jnp.concatenate([phonon_ref[:, at_before], phonon_ref[:, at_block], phonon_ref[:, at_after]], axis=1)
        rate = jnp.zeros(level.shape, jnp.float32)
        for k in range(LEVELS):
            rate = jnp.where(level == k, couplings_ref[k], rate)
        grown, shrunk = jnp.exp(rate), jnp.exp(-rate)
        cosh, sinh = 0.5 * (grown + shrunk), 0.5 * (grown - shrunk)
        cosh_left, sinh_left = pltpu.roll(cosh, 1, 1), pltpu.roll(sinh, 1, 1)
        even = lax.broadcasted_iota(jnp.int32, rate.shape, 1) % 2 == 0
        inside = slice(LANES, LANES + count)
        sign = (2 * fields_ref[:, at_block] - 1).astype(jnp.float32)
        scale = jnp.exp(hs_strength * sign)
        rows = [
            jnp.where(even, cosh, cosh_left)[:, inside],
            jnp.where(even, sinh, sinh_left)[:, inside],
            scale * jnp.where(even, cosh_left, cosh)[:, inside],
            scale * jnp.where(even, sinh_left, sinh)[:, inside],
            jnp.concatenate(
                [cosh[:, :LANES], cosh[:, LANES + count :], sinh[:, :LANES], sinh[:, LANES + count :]], axis=1
            ),
        ]
        for slice_no in range(turn, SLICES, 2):
            for k, row in enumerate(rows):
                out_ref[slice_no, k : k + 1, :] = row[slice_no : slice_no + 1]


def halves(x):
    high = x.astype(jnp.bfloat16)
    return high, (x - high.astype(jnp.float32)).astype(jnp.bfloat16)


def product(a, b, contract_b):
    dims = (((1,), (contract_b,)), ((), ()))
    dot = functools.partial(lax.dot_general, dimension_numbers=dims, preferred_element_type=jnp.float32)
    a_high, a_low = halves(a)
    b_high, b_low = halves(b)
    return dot(a_high, b_high) + (dot(a_high, b_low) + dot(a_low, b_high))


def mixed(w, u, rim, mix):
    before, after = LANES - 2, LANES
    rim_left = mix[4:5, before + 2 * LANES : before + 2 * LANES + 1] * rim[0] + mix[4:5, before : before + 1] * rim[1]
    rim_right = mix[4:5, after : after + 1] * rim[2] + mix[4:5, after + 2 * LANES : after + 2 * LANES + 1] * rim[3]
    end_left = jnp.sum(u * rim_left, axis=1, keepdims=True)
    end_right = jnp.sum(u * rim_right, axis=1, keepdims=True)
    count = w.shape[1]
    lane = lax.broadcasted_iota(jnp.int32, w.shape, 1)
    even = lane % 2 == 0
    partner = jnp.where(even, pltpu.roll(w, count - 1, 1), pltpu.roll(w, 1, 1))
    e = mix[0:1] * w + mix[1:2] * partner
    below = jnp.where(lane == 0, end_left, pltpu.roll(e, 1, 1))
    above = jnp.where(lane == count - 1, end_right, pltpu.roll(e, count - 1, 1))
    return mix[2:3] * e + mix[3:4] * jnp.where(even, below, above)


def joined(pieces):
    return jnp.concatenate(pieces, axis=1)


def in_rows(x, row):
    return [x[row : row + 1, k * LANES : (k + 1) * LANES] for k in range(x.shape[1] // LANES)]


def keep_rims(ref, rows):
    ref[...] = jnp.zeros(ref.shape, ref.dtype)
    for k, row in enumerate(rows):
        ref[k : k + 1, :] = row


def first_kernel(ids_ref, g_ref, mine_ref, other_ref, mix_ref, out_ref, rim_ref):
    core, row, z, high = ids_ref[0], ids_ref[1], ids_ref[2], ids_ref[3]
    peers = g_ref.shape[0] // 2
    width = mine_ref.shape[1]
    columns = peers * g_ref.shape[1]

    def of_core(k):
        return g_ref[pl.ds(k * peers, peers), :, 0:width].reshape(columns, width)

    w = product(of_core(core), mine_ref[...], 1) + product(of_core(1 - core), other_ref[...], 1)
    u = joined([of_core(0), of_core(1)])
    low, top = [], []
    for k in range(2):
        low.append(g_ref[k * peers + (row + peers - 1) % peers, :, width : width + LANES])
        top.append(g_ref[k * peers + (row + 1) % peers, :, width : width + LANES])
    rows = [
        joined([tile[2 * j + i : 2 * j + i + 1] for tile in tiles for i in range(2)])
        for tiles, start in ((low, 0), (top, 2))
        for j in (start, start + 1)
    ]
    keep_rims(rim_ref, rows)
    groups = out_ref.shape[0]
    out_ref[:, :, 0 : w.shape[1]] = mixed(w, u, rows, mix_ref[...]).reshape(groups, columns // groups, w.shape[1])

    upper = jnp.where(core == 1, mine_ref[:, width - LANES :], other_ref[:, width - LANES :]).T
    lower = jnp.where(core == 0, mine_ref[:, :LANES], other_ref[:, :LANES]).T
    tail = jnp.concatenate(in_rows(upper, LANES - 2) + in_rows(upper, LANES - 1), axis=0)
    head = jnp.concatenate(in_rows(lower, 0) + in_rows(lower, 1), axis=0)
    tail_to = (z + high) % groups
    head_to = (z + groups - 1 + high) % groups
    for p in range(groups):
        out_ref[p, 0:8, w.shape[1] :] = jnp.where(tail_to == p, tail, 0.0)
        out_ref[p, 8:16, w.shape[1] :] = jnp.where(head_to == p, head, 0.0)


def along_product(core, u, mine_ref, other_ref, w_ref):
    width = mine_ref.shape[1]
    w_ref[:, pl.ds(pl.multiple_of(core * width, width), width)] = product(u, mine_ref[...], 0)
    w_ref[:, pl.ds(pl.multiple_of((1 - core) * width, width), width)] = product(u, other_ref[...], 0)
    return w_ref[...]


def second_kernel(ids_ref, u_ref, ends_ref, mine_ref, other_ref, mix_ref, out_ref, rim_ref, w_ref):
    u = u_ref[...]
    w = along_product(ids_ref[0], u, mine_ref, other_ref, w_ref)
    rows = [joined([ends_ref[4 * j + k : 4 * j + k + 1, :] for k in range(4)]) for j in range(4)]
    keep_rims(rim_ref, rows)
    out_ref[...] = mixed(w, u, rows, mix_ref[...])


def third_kernel(ids_ref, u_ref, mine_ref, other_ref, rim_ref, mix_ref, out_ref):
    width = mine_ref.shape[1]
    core = ids_ref[0]
    u_mine = u_ref[:, pl.ds(pl.multiple_of(core * width, width), width)]
    u_other = u_ref[:, pl.ds(pl.multiple_of((1 - core) * width, width), width)]
    w = product(u_mine, mine_ref[...], 1) + product(u_other, other_ref[...], 1)
    rows = [rim_ref[k : k + 1, :] for k in range(4)]
    out_ref[...] = mixed(w, u_ref[...], rows, mix_ref[...])


def fourth_kernel(ids_ref, u_ref, mine_ref, other_ref, rim_ref, mix_ref, out_ref, w_ref):
    u = u_ref[...]
    w = along_product(ids_ref[0], u, mine_ref, other_ref, w_ref)
    rows = [rim_ref[k : k + 1, :] for k in range(4)]
    f = mixed(w, u, rows, mix_ref[...])
    width = out_ref.shape[2]
    peers = out_ref.shape[0] // 2
    for k in range(2):
        out_ref[k * peers : (k + 1) * peers] = f[:, k * width : (k + 1) * width].reshape(peers, 8, width)


def shards(propagator, slab, fields, phonon, couplings):
    block, width = propagator.shape
    count = 2 * width
    columns = slab.T
    half = columns.shape[0] // 2
    peers = lax.axis_size(ROW)
    groups = lax.axis_size("z")
    held = peers * half

    def full(*shape):
        return jax.ShapeDtypeStruct(shape, jnp.float32)

    mine = propagator
    other = swapped(propagator, "core")

    rims = jnp.concatenate([mine[-2:].reshape(4, LANES), mine[:2].reshape(4, LANES)])
    parts = jnp.stack([jnp.concatenate([columns[k * half : (k + 1) * half], rims], axis=1) for k in range(2)])
    parts = jnp.broadcast_to(parts[:, None], (2, peers, half, width + LANES))
    g = exchanged(parts.reshape(2 * peers, half, width + LANES), PAIRED_ROW)

    places = ("core", ROW, "z", "yhi")
    ids = jnp.stack([lax.axis_index(place) for place in places]).astype(jnp.int32)
    first = jnp.stack([lax.axis_index(ROW) * block, lax.axis_index(CUT) * count]).astype(jnp.int32)
    mix = call(
        mixing_kernel, "mixing", full(SLICES, 8, count), [SMEM, SMEM, VMEM, VMEM], size=4 * 10 * SITES
    )(first, couplings, phonon, fields)

    work = dict(flops=12 * held * block * count, size=8 * block * count)
    out, row_rim = call(
        first_kernel, "first", (full(groups, 2 * half, block + LANES), full(8, count)), [SMEM] + [VMEM] * 4, **work
    )(ids, g, mine, other, mix[0])
    share = exchanged(out, "z").sum(axis=0)
    across = swapped(share, "yhi")
    u = gathered(share[:, :block] + across[:, :block], "z")

    scratch = [pltpu.VMEM((held, count), jnp.float32)]
    w, cut_rim = call(
        second_kernel, "second", (full(held, count), full(8, block)), [SMEM] + [VMEM] * 5, scratch, **work
    )(ids, u, across[:, block:], mine, other, mix[1])
    u = gathered(summed(w, ROW), ROW)

    w = call(third_kernel, "third", full(held, block), [SMEM] + [VMEM] * 5, **work)(
        ids, u, mine, other, row_rim, mix[2]
    )
    share = summed(w, "z")
    u = gathered(share + swapped(share, "yhi"), "z")

    parts = call(
        fourth_kernel, "fourth", full(2 * peers, half, width), [SMEM] + [VMEM] * 5, scratch, **work
    )(ids, u, mine, other, cut_rim, mix[3])
    out = exchanged(parts, PAIRED_ROW).reshape(2, peers, half, width).sum(axis=1)
    return out.reshape(2 * half, width).T


def solution(mesh):
    devices = mesh.devices.reshape(8, 2, 2, 4, 4)
    fine = Mesh(devices, ("z", "yhi", "core", "x", "ylo"))
    cuts = ("z", "yhi", "core")
    in_specs = (P(ROW, cuts), P(cuts, ROW), P(), P(), P())
    return jax.shard_map(shards, mesh=fine, in_specs=in_specs, out_specs=P(cuts, ROW), check_vma=False)
```

time: 195 us -> 154 us (0.79)
  blocking collectives: 0 us -> 91 us
  starting transfers between devices: 81.6 us -> 24.5 us
  waiting for transfers between devices: 78.9 us -> 27.8 us
  other arithmetic: 15.8 us -> 0.87 us
  local copies, waits for them, and re-layouts: 10 us -> 2.91 us
    all_to_all x0 -> x6, blocking collectives: none -> 91 us  [exchanged(): return lax.all_to_all(parts, axes, 0, 0, tiled=True)]
    all_to_all x8 -> x2, waiting for transfers between devices: 63.9 us -> 18.5 us  [exchanged(): return lax.all_to_all(parts, axes, 0, 0, tiled=True)]
    all_to_all x8 -> x2, starting transfers between devices: 42.9 us -> 14.1 us  [exchanged(): return lax.all_to_all(parts, axes, 0, 0, tiled=True)]
    ppermute x7 -> x3, starting transfers between devices: 38.7 us -> 10.4 us  [swapped(): return lax.ppermute(x, axis, [(0, 1), (1, 0)])]
    ppermute x7 -> x3, waiting for transfers between devices: 15 us -> 9.29 us  [swapped(): return lax.ppermute(x, axis, [(0, 1), (1, 0)])]
    sinh x4 -> x0, other arithmetic: 5.49 us -> none  [mixing(): outer = jnp.concatenate([jnp.cosh(outer), jnp.sinh(outer)])]
    cosh x4 -> x0, other arithmetic: 5.49 us -> none  [mixing(): outer = jnp.concatenate([jnp.cosh(outer), jnp.sinh(outer)])]
    slice x8 -> x3, local copies, waits for them, and re-layouts: 5.13 us -> 0.73 us  [the longest x1 0.73 us: shards(): mine[-2:].reshape(4, LANES)]
  transfers between devices with their start and end apart: 15 -> 5, of which waited for: 10 -> 5; matrix products, arithmetic and copies ran while one was open for 11% -> 0% of each run, Pallas kernels for 0% -> 0%
where the time goes in v2:
time: 154 us
  blocking collectives  91 us (59%)
  waiting for transfers between devices  27.8 us (18%)
  starting transfers between devices  24.5 us (16%)
  Pallas kernels  6.45 us (4%)
  local copies, waits for them, and re-layouts  2.91 us (2%)
    all_to_all x6, blocking collectives, exchanged(): return lax.all_to_all(parts, axes, 0, 0, tiled=True)  91 us
    all_to_all x2, waiting for transfers between devices, exchanged(): return lax.all_to_all(parts, axes, 0, 0, tiled=True)  18.5 us
    all_to_all x2, starting transfers between devices, exchanged(): return lax.all_to_all(parts, axes, 0, 0, tiled=True)  14.1 us
    ppermute x3, starting transfers between devices, swapped(): return lax.ppermute(x, axis, [(0, 1), (1, 0)])  10.4 us
    ppermute x3, waiting for transfers between devices, swapped(): return lax.ppermute(x, axis, [(0, 1), (1, 0)])  9.29 us
  transfers between devices with their start and end apart: 5, of which 5 were waited for; matrix products, arithmetic and copies ran while one was open for 0% of the time, Pallas kernels for 0%

profile of v2, /device:TPU:1, one launch (start us, length us, event | category | flops | bytes accessed | tf_op | source)
XLA Modules:
  0.0 153.7 jit_solution(17532426371246468753)
XLA Ops:
  0.0 0.0 copy-start.4
  0.0 0.7 fusion.2
  0.8 0.0 copy-done.4
  0.8 0.0 copy-start
  0.8 0.8 broadcast_in_dim.8
  1.6 0.0 copy-start.1
  1.6 0.0 copy-start.2
  1.6 10.6 %all-to-all-start = ((f32[32,8,384]{2,1,0:T(8,128)}), f32[32,8,384]{2,1,0:T(8,128)S(1)}, u32[]{:S(2)}, u32[]{:S(2)}) async-start(f32[32,8,384]{2,1,0:T(8,128)} %bitcast.7), calls=%async_computation | async-start | bytes 786432 | tf_op jit(solution)/shard_map/all_to_all | solution.py:30
  12.2 0.0 copy-done
  12.2 2.2 %collective-permute-start = (f32[512,256]{1,0:T(8,128)S(1)}, f32[512,256]{1,0:T(8,128)S(1)}, u32[]{:S(2)}, u32[]{:S(2)}) collective-permute-start(f32[512,256]{1,0:T(8,128)S(1)} %copy-done), channel_id=1, source_target_pairs={{0,16},{16,0},{1,17},{17,1},{2,18},{18,2},{3,19},{19,3},{4,20},{20... | collective-permute-start | bytes 1572872 | tf_op jit(solution)/shard_map/ppermute | solution.py:26
  14.4 0.0 copy-start.3
  14.4 0.1 pad_add_fusion.1.first_ref
  14.5 0.0 copy-done.1
  14.5 0.0 copy-done.2
  14.5 0.6 copy-done.3
  15.0 0.7 mixing.1
  15.8 0.1 pad_add_fusion.ids_ref
  15.8 0.2 collective-permute-done.other_ref
  16.0 9.2 %all-to-all-done.g_ref = f32[32,8,384]{2,1,0:T(8,128)S(1)} async-done(((f32[32,8,384]{2,1,0:T(8,128)}), f32[32,8,384]{2,1,0:T(8,128)S(1)}, u32[]{:S(2)}, u32[]{:S(2)}) %all-to-all-start) | async-done | bytes 393248 | tf_op jit(solution)/shard_map/all_to_all | solution.py:30
  25.2 1.5 first.1
  26.7 19.3 %all_to_all.40 = f32[8,16,640]{2,1,0:T(8,128)S(1)} all-to-all(f32[8,16,640]{2,1,0:T(8,128)S(1)} %get-tuple-element.9), channel_id=1, replica_groups=mesh['z'=8,'yhi'=2,'core'=2,'x'=4,'ylo'=4] {'z'}, dimensions={0} | all-to-all | bytes 655360 | tf_op jit(solution)/shard_map/all_to_all | solution.py:30
  46.1 4.8 %collective-permute-start.1 = (f32[16,640]{1,0:T(8,128)S(1)}, f32[16,640]{1,0:T(8,128)S(1)}, u32[]{:S(2)}, u32[]{:S(2)}) collective-permute-start(f32[16,640]{1,0:T(8,128)S(1)} %reduce_sum.36), channel_id=1, source_target_pairs={{0,32},{32,0},{1,33},{33,1},{2,34},{34,2},{3,35},{35,3},{4,36},{36... | collective-permute-start | bytes 122888 | tf_op jit(solution)/shard_map/ppermute | solution.py:26
  50.8 3.9 %collective-permute-done.1 = f32[16,640]{1,0:T(8,128)S(1)} collective-permute-done((f32[16,640]{1,0:T(8,128)S(1)}, f32[16,640]{1,0:T(8,128)S(1)}, u32[]{:S(2)}, u32[]{:S(2)}) %collective-permute-start.1) | collective-permute-done | bytes 40992 | tf_op jit(solution)/shard_map/ppermute | solution.py:26
  54.7 0.7 broadcast_in_dim.9
  55.5 3.5 %all-to-all-start.2 = ((f32[8,16,512]{2,1,0:T(8,128)}), f32[8,16,512]{2,1,0:T(8,128)S(1)}, u32[]{:S(2)}, u32[]{:S(2)}) async-start(f32[8,16,512]{2,1,0:T(8,128)} %broadcast_in_dim.9), calls=%async_computation.2 | async-start | bytes 524288 | tf_op jit(solution)/shard_map/all_to_all | solution.py:30
  59.0 9.3 %all-to-all-done.2 = f32[8,16,512]{2,1,0:T(8,128)S(1)} async-done(((f32[8,16,512]{2,1,0:T(8,128)}), f32[8,16,512]{2,1,0:T(8,128)S(1)}, u32[]{:S(2)}, u32[]{:S(2)}) %all-to-all-start.2) | async-done | bytes 262176 | tf_op jit(solution)/shard_map/all_to_all | solution.py:30
  68.3 1.4 second.1
  69.7 14.4 %all_to_all.41 = f32[16,8,512]{2,1,0:T(8,128)S(1)} all-to-all(f32[16,8,512]{2,1,0:T(8,128)S(1)} %bitcast.34), channel_id=1, replica_groups=mesh['z'=8,'yhi'=2,'core'=2,'x'=4,'ylo'=4] {'x','ylo'}, dimensions={0} | all-to-all | bytes 524288 | tf_op jit(solution)/shard_map/all_to_all | solution.py:30
  84.1 10.9 %all_to_all.42 = f32[16,8,512]{2,1,0:T(8,128)S(1)} all-to-all(f32[16,8,512]{2,1,0:T(8,128)S(1)} %broadcast_in_dim.10), channel_id=1, replica_groups=mesh['z'=8,'yhi'=2,'core'=2,'x'=4,'ylo'=4] {'x','ylo'}, dimensions={0} | all-to-all | bytes 524288 | tf_op jit(solution)/shard_map/all_to_all | solution.py:30
  95.0 1.5 third.1
  96.5 13.5 %all_to_all.43 = f32[8,16,512]{2,1,0:T(8,128)S(1)} all-to-all(f32[8,16,512]{2,1,0:T(8,128)S(1)} %bitcast.32), channel_id=1, replica_groups=mesh['z'=8,'yhi'=2,'core'=2,'x'=4,'ylo'=4] {'z'}, dimensions={0} | all-to-all | bytes 524288 | tf_op jit(solution)/shard_map/all_to_all | solution.py:30
  110.0 3.5 %collective-permute-start.2 = (f32[16,512]{1,0:T(8,128)S(1)}, f32[16,512]{1,0:T(8,128)S(1)}, u32[]{:S(2)}, u32[]{:S(2)}) collective-permute-start(f32[16,512]{1,0:T(8,128)S(1)} %reduce_sum.38), channel_id=1, source_target_pairs={{0,32},{32,0},{1,33},{33,1},{2,34},{34,2},{3,35},{35,3},{4,36},{36... | collective-permute-start | bytes 98312 | tf_op jit(solution)/shard_map/ppermute | solution.py:26
  113.5 5.2 %collective-permute-done.2 = f32[16,512]{1,0:T(8,128)S(1)} collective-permute-done((f32[16,512]{1,0:T(8,128)S(1)}, f32[16,512]{1,0:T(8,128)S(1)}, u32[]{:S(2)}, u32[]{:S(2)}) %collective-permute-start.2) | collective-permute-done | bytes 32800 | tf_op jit(solution)/shard_map/ppermute | solution.py:26
  118.7 11.7 %all_to_all.44 = f32[8,16,512]{2,1,0:T(8,128)S(1)} all-to-all(f32[8,16,512]{2,1,0:T(8,128)S(1)} %broadcast_in_dim.11), channel_id=1, replica_groups=mesh['z'=8,'yhi'=2,'core'=2,'x'=4,'ylo'=4] {'z'}, dimensions={0} | all-to-all | bytes 524288 | tf_op jit(solution)/shard_map/all_to_all | solution.py:30
  130.5 1.4 fourth.1
  131.8 21.2 %all_to_all.45 = f32[32,8,256]{2,1,0:T(8,128)S(1)} all-to-all(f32[32,8,256]{2,1,0:T(8,128)S(1)} %fourth.1), channel_id=1, replica_groups=mesh['z'=8,'yhi'=2,'core'=2,'x'=4,'ylo'=4] {'core','x','ylo'}, dimensions={0} | all-to-all | bytes 524288 | tf_op jit(solution)/shard_map/all_to_all | solution.py:30
  153.0 0.6 bitcast_reduce_fusion
  (14 shorter events, 0.2 us)
Async XLA Ops:
  0.0 0.8 copy-start.4
  0.8 11.4 %copy-start = (f32[512,256]{1,0:T(8,128)S(1)}, f32[512,256]{1,0:T(8,128)}, u32[]{:S(2)}) copy-start(f32[512,256]{1,0:T(8,128)} %mine_ref.7) | copy-start | bytes 1572868
  1.6 12.9 %copy-start.1 = (s32[4,8192]{1,0:T(4,128)S(1)}, s32[4,8192]{1,0:T(4,128)}, u32[]{:S(2)}) copy-start(s32[4,8192]{1,0:T(4,128)} %phonon_ref.1) | copy-start | bytes 393220
  1.6 12.9 %copy-start.2 = (s32[4,8192]{1,0:T(4,128)S(1)}, s32[4,8192]{1,0:T(4,128)}, u32[]{:S(2)}) copy-start(s32[4,8192]{1,0:T(4,128)} %fields_ref.1) | copy-start | bytes 393220
  1.6 23.6 %all-to-all-start = ((f32[32,8,384]{2,1,0:T(8,128)}), f32[32,8,384]{2,1,0:T(8,128)S(1)}, u32[]{:S(2)}, u32[]{:S(2)}) async-start(f32[32,8,384]{2,1,0:T(8,128)} %bitcast.7), calls=%async_computation | async-start | bytes 786432 | tf_op jit(solution)/shard_map/all_to_all | solution.py:30
  12.2 3.8 %collective-permute-start = (f32[512,256]{1,0:T(8,128)S(1)}, f32[512,256]{1,0:T(8,128)S(1)}, u32[]{:S(2)}, u32[]{:S(2)}) collective-permute-start(f32[512,256]{1,0:T(8,128)S(1)} %copy-done), channel_id=1, source_target_pairs={{0,16},{16,0},{1,17},{17,1},{2,18},{18,2},{3,19},{19,3},{4,20},{20... | collective-permute-start | bytes 1572872 | tf_op jit(solution)/shard_map/ppermute | solution.py:26
  14.4 0.7 copy-start.3
  46.1 8.7 %collective-permute-start.1 = (f32[16,640]{1,0:T(8,128)S(1)}, f32[16,640]{1,0:T(8,128)S(1)}, u32[]{:S(2)}, u32[]{:S(2)}) collective-permute-start(f32[16,640]{1,0:T(8,128)S(1)} %reduce_sum.36), channel_id=1, source_target_pairs={{0,32},{32,0},{1,33},{33,1},{2,34},{34,2},{3,35},{35,3},{4,36},{36... | collective-permute-start | bytes 122888 | tf_op jit(solution)/shard_map/ppermute | solution.py:26
  55.5 12.8 %all-to-all-start.2 = ((f32[8,16,512]{2,1,0:T(8,128)}), f32[8,16,512]{2,1,0:T(8,128)S(1)}, u32[]{:S(2)}, u32[]{:S(2)}) async-start(f32[8,16,512]{2,1,0:T(8,128)} %broadcast_in_dim.9), calls=%async_computation.2 | async-start | bytes 524288 | tf_op jit(solution)/shard_map/all_to_all | solution.py:30
  110.0 8.7 %collective-permute-start.2 = (f32[16,512]{1,0:T(8,128)S(1)}, f32[16,512]{1,0:T(8,128)S(1)}, u32[]{:S(2)}, u32[]{:S(2)}) collective-permute-start(f32[16,512]{1,0:T(8,128)S(1)} %reduce_sum.38), channel_id=1, source_target_pairs={{0,32},{32,0},{1,33},{33,1},{2,34},{34,2},{3,35},{35,3},{4,36},{36... | collective-permute-start | bytes 98312 | tf_op jit(solution)/shard_map/ppermute | solution.py:26

commit v3 on v2

--- a/solution.py
+++ b/solution.py
@@ -91,12 +91,18 @@
     return high, (x - high.astype(jnp.float32)).astype(jnp.bfloat16)
 
 
-def product(a, b, contract_b):
+def split_kernel(mine_ref, other_ref, *out_refs):
+    for k, ref in enumerate((mine_ref, other_ref)):
+        out_refs[2 * k][...], out_refs[2 * k + 1][...] = halves(ref[...])
+
+
+def product(a, b_high_ref, b_low_ref, contract_b):
     dims = (((1,), (contract_b,)), ((), ()))
     dot = functools.partial(lax.dot_general, dimension_numbers=dims, preferred_element_type=jnp.float32)
     a_high, a_low = halves(a)
-    b_high, b_low = halves(b)
-    return dot(a_high, b_high) + (dot(a_high, b_low) + dot(a_low, b_high))
+    both = dot(jnp.concatenate([a_high, a_low], axis=0), b_high_ref[...])
+    count = a.shape[0]
+    return both[:count] + (both[count:] + dot(a_high, b_low_ref[...]))
 
 
 def mixed(w, u, rim, mix):
@@ -129,7 +135,7 @@
         ref[k : k + 1, :] = row
 
 
-def first_kernel(ids_ref, g_ref, mine_ref, other_ref, mix_ref, out_ref, rim_ref):
+def first_kernel(ids_ref, g_ref, mine_ref, other_ref, mh_ref, ml_ref, oh_ref, ol_ref, mix_ref, out_ref, rim_ref):
     core, row, z, high = ids_ref[0], ids_ref[1], ids_ref[2], ids_ref[3]
     peers = g_ref.shape[0] // 2
     width = mine_ref.shape[1]
@@ -138,7 +144,7 @@
     def of_core(k):
         return g_ref[pl.ds(k * peers, peers), :, 0:width].reshape(columns, width)
 
-    w = product(of_core(core), mine_ref[...], 1) + product(of_core(1 - core), other_ref[...], 1)
+    w = product(of_core(core), mh_ref, ml_ref, 1) + product(of_core(1 - core), oh_ref, ol_ref, 1)
     u = joined([of_core(0), of_core(1)])
     low, top = [], []
     for k in range(2):
@@ -151,7 +157,7 @@
     ]
     keep_rims(rim_ref, rows)
     groups = out_ref.shape[0]
-    out_ref[:, :, 0 : w.shape[1]] = mixed(w, u, rows, mix_ref[...]).reshape(groups, columns // groups, w.shape[1])
+    out_ref[:, :, 0 : w.shape[1]] = mixed(w, u, rows, mix_ref[0]).reshape(groups, columns // groups, w.shape[1])
 
     upper = jnp.where(core == 1, mine_ref[:, width - LANES :], other_ref[:, width - LANES :]).T
     lower = jnp.where(core == 0, mine_ref[:, :LANES], other_ref[:, :LANES]).T
@@ -164,36 +170,37 @@
         out_ref[p, 8:16, w.shape[1] :] = jnp.where(head_to == p, head, 0.0)
 
 
-def along_product(core, u, mine_ref, other_ref, w_ref):
-    width = mine_ref.shape[1]
-    w_ref[:, pl.ds(pl.multiple_of(core * width, width), width)] = product(u, mine_ref[...], 0)
-    w_ref[:, pl.ds(pl.multiple_of((1 - core) * width, width), width)] = product(u, other_ref[...], 0)
+def along_product(core, u, mh_ref, ml_ref, oh_ref, ol_ref, w_ref):
+    width = mh_ref.shape[1]
+    w_ref[:, pl.ds(pl.multiple_of(core * width, width), width)] = product(u, mh_ref, ml_ref, 0)
+    w_ref[:, pl.ds(pl.multiple_of((1 - core) * width, width), width)] = product(u, oh_ref, ol_ref, 0)
     return w_ref[...]
 
 
-def second_kernel(ids_ref, u_ref, ends_ref, mine_ref, other_ref, mix_ref, out_ref, rim_ref, w_ref):
+def second_kernel(ids_ref, u_ref, ends_ref, mh_ref, ml_ref, oh_ref, ol_ref, mix_ref, out_ref, rim_ref, w_ref):
     u = u_ref[...]
-    w = along_product(ids_ref[0], u, mine_ref, other_ref, w_ref)
-    rows = [joined([ends_ref[4 * j + k : 4 * j + k + 1, :] for k in range(4)]) for j in range(4)]
+    w = along_product(ids_ref[0], u, mh_ref, ml_ref, oh_ref, ol_ref, w_ref)
+    at = u.shape[1]
+    rows = [joined([ends_ref[4 * j + k : 4 * j + k + 1, at : at + LANES] for k in range(4)]) for j in range(4)]
     keep_rims(rim_ref, rows)
-    out_ref[...] = mixed(w, u, rows, mix_ref[...])
-
-
-def third_kernel(ids_ref, u_ref, mine_ref, other_ref, rim_ref, mix_ref, out_ref):
-    width = mine_ref.shape[1]
+    out_ref[...] = mixed(w, u, rows, mix_ref[1])
+
+
+def third_kernel(ids_ref, u_ref, mh_ref, ml_ref, oh_ref, ol_ref, rim_ref, mix_ref, out_ref):
+    width = mh_ref.shape[1]
     core = ids_ref[0]
     u_mine = u_ref[:, pl.ds(pl.multiple_of(core * width, width), width)]
     u_other = u_ref[:, pl.ds(pl.multiple_of((1 - core) * width, width), width)]
-    w = product(u_mine, mine_ref[...], 1) + product(u_other, other_ref[...], 1)
+    w = product(u_mine, mh_ref, ml_ref, 1) + product(u_other, oh_ref, ol_ref, 1)
     rows = [rim_ref[k : k + 1, :] for k in range(4)]
-    out_ref[...] = mixed(w, u_ref[...], rows, mix_ref[...])
-
-
-def fourth_kernel(ids_ref, u_ref, mine_ref, other_ref, rim_ref, mix_ref, out_ref, w_ref):
+    out_ref[...] = mixed(w, u_ref[...], rows, mix_ref[2])
+
+
+def fourth_kernel(ids_ref, u_ref, mh_ref, ml_ref, oh_ref, ol_ref, rim_ref, mix_ref, out_ref, w_ref):
     u = u_ref[...]
-    w = along_product(ids_ref[0], u, mine_ref, other_ref, w_ref)
+    w = along_product(ids_ref[0], u, mh_ref, ml_ref, oh_ref, ol_ref, w_ref)
     rows = [rim_ref[k : k + 1, :] for k in range(4)]
-    f = mixed(w, u, rows, mix_ref[...])
+    f = mixed(w, u, rows, mix_ref[3])
     width = out_ref.shape[2]
     peers = out_ref.shape[0] // 2
     for k in range(2):
@@ -227,29 +234,32 @@
         mixing_kernel, "mixing", full(SLICES, 8, count), [SMEM, SMEM, VMEM, VMEM], size=4 * 10 * SITES
     )(first, couplings, phonon, fields)
 
+    split = jax.ShapeDtypeStruct((block, width), jnp.bfloat16)
+    pieces = call(split_kernel, "split", (split,) * 4, [VMEM, VMEM], size=16 * block * width)(mine, other)
+
     work = dict(flops=12 * held * block * count, size=8 * block * count)
     out, row_rim = call(
-        first_kernel, "first", (full(groups, 2 * half, block + LANES), full(8, count)), [SMEM] + [VMEM] * 4, **work
-    )(ids, g, mine, other, mix[0])
+        first_kernel, "first", (full(groups, 2 * half, block + LANES), full(8, count)), [SMEM] + [VMEM] * 8, **work
+    )(ids, g, mine, other, *pieces, mix)
     share = exchanged(out, "z").sum(axis=0)
     across = swapped(share, "yhi")
     u = gathered(share[:, :block] + across[:, :block], "z")
 
     scratch = [pltpu.VMEM((held, count), jnp.float32)]
     w, cut_rim = call(
-        second_kernel, "second", (full(held, count), full(8, block)), [SMEM] + [VMEM] * 5, scratch, **work
-    )(ids, u, across[:, block:], mine, other, mix[1])
+        second_kernel, "second", (full(held, count), full(8, block)), [SMEM] + [VMEM] * 7, scratch, **work
+    )(ids, u, across, *pieces, mix)
     u = gathered(summed(w, ROW), ROW)
 
-    w = call(third_kernel, "third", full(held, block), [SMEM] + [VMEM] * 5, **work)(
-        ids, u, mine, other, row_rim, mix[2]
+    w = call(third_kernel, "third", full(held, block), [SMEM] + [VMEM] * 7, **work)(
+        ids, u, *pieces, row_rim, mix
     )
     share = summed(w, "z")
     u = gathered(share + swapped(share, "yhi"), "z")
 
     parts = call(
-        fourth_kernel, "fourth", full(2 * peers, half, width), [SMEM] + [VMEM] * 5, scratch, **work
-    )(ids, u, mine, other, cut_rim, mix[3])
+        fourth_kernel, "fourth", full(2 * peers, half, width), [SMEM] + [VMEM] * 7, scratch, **work
+    )(ids, u, *pieces, cut_rim, mix)
     out = exchanged(parts, PAIRED_ROW).reshape(2, peers, half, width).sum(axis=1)
     return out.reshape(2 * half, width).T
 

time: 154 us -> 152 us (0.987)
  blocking collectives: 91 us -> 103 us
  waiting for transfers between devices: 27.8 us -> 17.3 us
  starting transfers between devices: 24.5 us -> 21.9 us
    all_to_all x6 -> x7, blocking collectives: 91 us -> 103 us  [exchanged(): return lax.all_to_all(parts, axes, 0, 0, tiled=True)]
    all_to_all x2 -> x1, waiting for transfers between devices: 18.5 us -> 8.96 us  [exchanged(): return lax.all_to_all(parts, axes, 0, 0, tiled=True)]
    all_to_all x2 -> x1, starting transfers between devices: 14.1 us -> 10.6 us  [exchanged(): return lax.all_to_all(parts, axes, 0, 0, tiled=True)]
  transfers between devices with their start and end apart: 5 -> 4, of which waited for: 5 -> 4; matrix products, arithmetic and copies ran while one was open for 0% -> 0% of each run, Pallas kernels for 0% -> 1%
where the time goes in v3:
time: 152 us
  blocking collectives  103 us (68%)
  starting transfers between devices  21.9 us (14%)
  waiting for transfers between devices  17.3 us (11%)
  Pallas kernels  6.19 us (4%)
  local copies, waits for them, and re-layouts  2.18 us (1%)
    all_to_all x7, blocking collectives, exchanged(): return lax.all_to_all(parts, axes, 0, 0, tiled=True)  103 us
    ppermute x3, starting transfers between devices, swapped(): return lax.ppermute(x, axis, [(0, 1), (1, 0)])  11.3 us
    all_to_all x1, starting transfers between devices, exchanged(): return lax.all_to_all(parts, axes, 0, 0, tiled=True)  10.6 us
    all_to_all x1, waiting for transfers between devices, exchanged(): return lax.all_to_all(parts, axes, 0, 0, tiled=True)  8.96 us
    ppermute x3, waiting for transfers between devices, swapped(): return lax.ppermute(x, axis, [(0, 1), (1, 0)])  8.29 us
  transfers between devices with their start and end apart: 4, of which 4 were waited for; matrix products, arithmetic and copies ran while one was open for 0% of the time, Pallas kernels for 1%

profile of v3, /device:TPU:1, one launch (start us, length us, event | category | flops | bytes accessed | tf_op | source)
XLA Modules:
  0.0 151.6 jit_solution(5391460156417197266)
XLA Ops:
  0.0 0.0 copy-start.4
  0.0 0.7 fusion.2
  0.8 0.0 copy-done.4
  0.8 0.0 copy-start
  0.8 0.8 broadcast_in_dim.8
  1.6 0.0 copy-start.1
  1.6 0.0 copy-start.2
  1.6 10.6 %all-to-all-start = ((f32[32,8,384]{2,1,0:T(8,128)}), f32[32,8,384]{2,1,0:T(8,128)S(1)}, u32[]{:S(2)}, u32[]{:S(2)}) async-start(f32[32,8,384]{2,1,0:T(8,128)} %bitcast.7), calls=%async_computation | async-start | bytes 786432 | tf_op jit(solution)/shard_map/all_to_all | solution.py:30
  12.2 0.0 copy-done
  12.2 2.2 %collective-permute-start = (f32[512,256]{1,0:T(8,128)S(1)}, f32[512,256]{1,0:T(8,128)S(1)}, u32[]{:S(2)}, u32[]{:S(2)}) collective-permute-start(f32[512,256]{1,0:T(8,128)S(1)} %copy-done), channel_id=1, source_target_pairs={{0,16},{16,0},{1,17},{17,1},{2,18},{18,2},{3,19},{19,3},{4,20},{20... | collective-permute-start | bytes 1572872 | tf_op jit(solution)/shard_map/ppermute | solution.py:26
  14.4 0.0 copy-start.3
  14.4 0.1 pad_add_fusion.1.first_ref
  14.5 0.0 copy-done.1
  14.5 0.0 copy-done.2
  14.5 0.6 copy-done.3
  15.0 0.7 mixing.1.mix_ref
  15.7 0.1 pad_add_fusion.ids_ref
  15.8 0.2 collective-permute-done.other_ref
  16.0 0.2 split.1
  16.2 9.0 %all-to-all-done.g_ref = f32[32,8,384]{2,1,0:T(8,128)S(1)} async-done(((f32[32,8,384]{2,1,0:T(8,128)}), f32[32,8,384]{2,1,0:T(8,128)S(1)}, u32[]{:S(2)}, u32[]{:S(2)}) %all-to-all-start) | async-done | bytes 393248 | tf_op jit(solution)/shard_map/all_to_all | solution.py:30
  25.2 1.4 first.1
  26.5 19.3 %all_to_all.40 = f32[8,16,640]{2,1,0:T(8,128)S(1)} all-to-all(f32[8,16,640]{2,1,0:T(8,128)S(1)} %get-tuple-element.17), channel_id=1, replica_groups=mesh['z'=8,'yhi'=2,'core'=2,'x'=4,'ylo'=4] {'z'}, dimensions={0} | all-to-all | bytes 655360 | tf_op jit(solution)/shard_map/all_to_all | solution.py:30
  45.9 4.8 %collective-permute-start.1 = (f32[16,640]{1,0:T(8,128)S(1)}, f32[16,640]{1,0:T(8,128)S(1)}, u32[]{:S(2)}, u32[]{:S(2)}) collective-permute-start(f32[16,640]{1,0:T(8,128)S(1)} %reduce_sum.36), channel_id=1, source_target_pairs={{0,32},{32,0},{1,33},{33,1},{2,34},{34,2},{3,35},{35,3},{4,36},{36... | collective-permute-start | bytes 122888 | tf_op jit(solution)/shard_map/ppermute | solution.py:26
  50.6 3.9 %collective-permute-done.1.ends_ref = f32[16,640]{1,0:T(8,128)S(1)} collective-permute-done((f32[16,640]{1,0:T(8,128)S(1)}, f32[16,640]{1,0:T(8,128)S(1)}, u32[]{:S(2)}, u32[]{:S(2)}) %collective-permute-start.1) | collective-permute-done | bytes 40992 | tf_op jit(solution)/shard_map/ppermute | solution.py:26
  54.6 12.7 %all_to_all.41 = f32[8,16,512]{2,1,0:T(8,128)S(1)} all-to-all(f32[8,16,512]{2,1,0:T(8,128)S(1)} %broadcast_in_dim.9), channel_id=1, replica_groups=mesh['z'=8,'yhi'=2,'core'=2,'x'=4,'ylo'=4] {'z'}, dimensions={0} | all-to-all | bytes 524288 | tf_op jit(solution)/shard_map/all_to_all | solution.py:30
  67.3 1.3 second.1
  68.6 13.5 %all_to_all.42 = f32[16,8,512]{2,1,0:T(8,128)S(1)} all-to-all(f32[16,8,512]{2,1,0:T(8,128)S(1)} %bitcast.26), channel_id=1, replica_groups=mesh['z'=8,'yhi'=2,'core'=2,'x'=4,'ylo'=4] {'x','ylo'}, dimensions={0} | all-to-all | bytes 524288 | tf_op jit(solution)/shard_map/all_to_all | solution.py:30
  82.2 10.9 %all_to_all.43 = f32[16,8,512]{2,1,0:T(8,128)S(1)} all-to-all(f32[16,8,512]{2,1,0:T(8,128)S(1)} %broadcast_in_dim.10), channel_id=1, replica_groups=mesh['z'=8,'yhi'=2,'core'=2,'x'=4,'ylo'=4] {'x','ylo'}, dimensions={0} | all-to-all | bytes 524288 | tf_op jit(solution)/shard_map/all_to_all | solution.py:30
  93.1 1.3 third.1
  94.5 13.3 %all_to_all.44 = f32[8,16,512]{2,1,0:T(8,128)S(1)} all-to-all(f32[8,16,512]{2,1,0:T(8,128)S(1)} %bitcast.24), channel_id=1, replica_groups=mesh['z'=8,'yhi'=2,'core'=2,'x'=4,'ylo'=4] {'z'}, dimensions={0} | all-to-all | bytes 524288 | tf_op jit(solution)/shard_map/all_to_all | solution.py:30
  107.8 4.3 %collective-permute-start.2 = (f32[16,512]{1,0:T(8,128)S(1)}, f32[16,512]{1,0:T(8,128)S(1)}, u32[]{:S(2)}, u32[]{:S(2)}) collective-permute-start(f32[16,512]{1,0:T(8,128)S(1)} %reduce_sum.38), channel_id=1, source_target_pairs={{0,32},{32,0},{1,33},{33,1},{2,34},{34,2},{3,35},{35,3},{4,36},{36... | collective-permute-start | bytes 98312 | tf_op jit(solution)/shard_map/ppermute | solution.py:26
  112.2 4.2 %collective-permute-done.2 = f32[16,512]{1,0:T(8,128)S(1)} collective-permute-done((f32[16,512]{1,0:T(8,128)S(1)}, f32[16,512]{1,0:T(8,128)S(1)}, u32[]{:S(2)}, u32[]{:S(2)}) %collective-permute-start.2) | collective-permute-done | bytes 32800 | tf_op jit(solution)/shard_map/ppermute | solution.py:26
  116.4 11.7 %all_to_all.45 = f32[8,16,512]{2,1,0:T(8,128)S(1)} all-to-all(f32[8,16,512]{2,1,0:T(8,128)S(1)} %broadcast_in_dim.11), channel_id=1, replica_groups=mesh['z'=8,'yhi'=2,'core'=2,'x'=4,'ylo'=4] {'z'}, dimensions={0} | all-to-all | bytes 524288 | tf_op jit(solution)/shard_map/all_to_all | solution.py:30
  128.2 1.3 fourth.1
  129.5 21.4 %all_to_all.46 = f32[32,8,256]{2,1,0:T(8,128)S(1)} all-to-all(f32[32,8,256]{2,1,0:T(8,128)S(1)} %fourth.1), channel_id=1, replica_groups=mesh['z'=8,'yhi'=2,'core'=2,'x'=4,'ylo'=4] {'core','x','ylo'}, dimensions={0} | all-to-all | bytes 524288 | tf_op jit(solution)/shard_map/all_to_all | solution.py:30
  150.9 0.6 bitcast_reduce_fusion
  (13 shorter events, 0.2 us)
Async XLA Ops:
  0.0 0.8 copy-start.4
  0.8 11.4 %copy-start = (f32[512,256]{1,0:T(8,128)S(1)}, f32[512,256]{1,0:T(8,128)}, u32[]{:S(2)}) copy-start(f32[512,256]{1,0:T(8,128)} %mine_ref.3) | copy-start | bytes 1572868
  1.6 12.9 %copy-start.1 = (s32[4,8192]{1,0:T(4,128)S(1)}, s32[4,8192]{1,0:T(4,128)}, u32[]{:S(2)}) copy-start(s32[4,8192]{1,0:T(4,128)} %phonon_ref.1) | copy-start | bytes 393220
  1.6 12.9 %copy-start.2 = (s32[4,8192]{1,0:T(4,128)S(1)}, s32[4,8192]{1,0:T(4,128)}, u32[]{:S(2)}) copy-start(s32[4,8192]{1,0:T(4,128)} %fields_ref.1) | copy-start | bytes 393220
  1.6 23.6 %all-to-all-start = ((f32[32,8,384]{2,1,0:T(8,128)}), f32[32,8,384]{2,1,0:T(8,128)S(1)}, u32[]{:S(2)}, u32[]{:S(2)}) async-start(f32[32,8,384]{2,1,0:T(8,128)} %bitcast.7), calls=%async_computation | async-start | bytes 786432 | tf_op jit(solution)/shard_map/all_to_all | solution.py:30
  12.2 3.8 %collective-permute-start = (f32[512,256]{1,0:T(8,128)S(1)}, f32[512,256]{1,0:T(8,128)S(1)}, u32[]{:S(2)}, u32[]{:S(2)}) collective-permute-start(f32[512,256]{1,0:T(8,128)S(1)} %copy-done), channel_id=1, source_target_pairs={{0,16},{16,0},{1,17},{17,1},{2,18},{18,2},{3,19},{19,3},{4,20},{20... | collective-permute-start | bytes 1572872 | tf_op jit(solution)/shard_map/ppermute | solution.py:26
  14.4 0.7 copy-start.3
  45.9 8.7 %collective-permute-start.1 = (f32[16,640]{1,0:T(8,128)S(1)}, f32[16,640]{1,0:T(8,128)S(1)}, u32[]{:S(2)}, u32[]{:S(2)}) collective-permute-start(f32[16,640]{1,0:T(8,128)S(1)} %reduce_sum.36), channel_id=1, source_target_pairs={{0,32},{32,0},{1,33},{33,1},{2,34},{34,2},{3,35},{35,3},{4,36},{36... | collective-permute-start | bytes 122888 | tf_op jit(solution)/shard_map/ppermute | solution.py:26
  107.8 8.6 %collective-permute-start.2 = (f32[16,512]{1,0:T(8,128)S(1)}, f32[16,512]{1,0:T(8,128)S(1)}, u32[]{:S(2)}, u32[]{:S(2)}) collective-permute-start(f32[16,512]{1,0:T(8,128)S(1)} %reduce_sum.38), channel_id=1, source_target_pairs={{0,32},{32,0},{1,33},{33,1},{2,34},{34,2},{3,35},{35,3},{4,36},{36... | collective-permute-start | bytes 98312 | tf_op jit(solution)/shard_map/ppermute | solution.py:26

commit v4 on v3

--- a/solution.py
+++ b/solution.py
@@ -30,10 +30,12 @@
     return lax.all_to_all(parts, axes, 0, 0, tiled=True)
 
 
+def from_all(x, axes):
+    return exchanged(jnp.broadcast_to(x[None], (lax.axis_size(axes), *x.shape)), axes)
+
+
 def gathered(x, axes):
-    count = lax.axis_size(axes)
-    parts = exchanged(jnp.broadcast_to(x[None], (count, *x.shape)), axes)
-    return parts.reshape(count * x.shape[0], x.shape[1])
+    return from_all(x, axes).reshape(-1, x.shape[1])
 
 
 def summed(x, axes):
@@ -135,6 +137,15 @@
         ref[k : k + 1, :] = row
 
 
+def pack_kernel(columns_ref, low_ref, high_ref, out_ref):
+    ends = in_rows(high_ref, 6) + in_rows(high_ref, 7) + in_rows(low_ref, 0) + in_rows(low_ref, 1)
+    rims = jnp.concatenate(ends, axis=0)
+    peers, half = out_ref.shape[0] // 2, out_ref.shape[1]
+    for k in range(2):
+        part = joined([columns_ref[k * half : (k + 1) * half, :], rims])
+        out_ref[k * peers : (k + 1) * peers] = jnp.broadcast_to(part[None], (peers, *part.shape))
+
+
 def first_kernel(ids_ref, g_ref, mine_ref, other_ref, mh_ref, ml_ref, oh_ref, ol_ref, mix_ref, out_ref, rim_ref):
     core, row, z, high = ids_ref[0], ids_ref[1], ids_ref[2], ids_ref[3]
     peers = g_ref.shape[0] // 2
@@ -180,8 +191,8 @@
 def second_kernel(ids_ref, u_ref, ends_ref, mh_ref, ml_ref, oh_ref, ol_ref, mix_ref, out_ref, rim_ref, w_ref):
     u = u_ref[...]
     w = along_product(ids_ref[0], u, mh_ref, ml_ref, oh_ref, ol_ref, w_ref)
-    at = u.shape[1]
-    rows = [joined([ends_ref[4 * j + k : 4 * j + k + 1, at : at + LANES] for k in range(4)]) for j in range(4)]
+    ends = ends_ref[1 - ids_ref[3], :, u.shape[1] :]
+    rows = [joined([ends[4 * j + k : 4 * j + k + 1] for k in range(4)]) for j in range(4)]
     keep_rims(rim_ref, rows)
     out_ref[...] = mixed(w, u, rows, mix_ref[1])
 
@@ -222,10 +233,21 @@
     mine = propagator
     other = swapped(propagator, "core")
 
-    rims = jnp.concatenate([mine[-2:].reshape(4, LANES), mine[:2].reshape(4, LANES)])
-    parts = jnp.stack([jnp.concatenate([columns[k * half : (k + 1) * half], rims], axis=1) for k in range(2)])
-    parts = jnp.broadcast_to(parts[:, None], (2, peers, half, width + LANES))
-    g = exchanged(parts.reshape(2 * peers, half, width + LANES), PAIRED_ROW)
+    parts = full(2 * peers, half, width + LANES)
+    parts = pl.pallas_call(
+        pack_kernel,
+        grid=(1,),
+        out_shape=parts,
+        in_specs=[
+            pl.BlockSpec(columns.shape, lambda i: (0, 0)),
+            pl.BlockSpec((8, width), lambda i: (0, 0)),
+            pl.BlockSpec((8, width), lambda i: (block // 8 - 1, 0)),
+        ],
+        out_specs=pl.BlockSpec(parts.shape, lambda i: (0, 0, 0)),
+        compiler_params=pltpu.CompilerParams(vmem_limit_bytes=60 * 1024 * 1024),
+        name="pack",
+    )(columns, mine, mine)
+    g = exchanged(parts, PAIRED_ROW)
 
     places = ("core", ROW, "z", "yhi")
     ids = jnp.stack([lax.axis_index(place) for place in places]).astype(jnp.int32)
@@ -242,20 +264,20 @@
         first_kernel, "first", (full(groups, 2 * half, block + LANES), full(8, count)), [SMEM] + [VMEM] * 8, **work
     )(ids, g, mine, other, *pieces, mix)
     share = exchanged(out, "z").sum(axis=0)
-    across = swapped(share, "yhi")
-    u = gathered(share[:, :block] + across[:, :block], "z")
+    both = from_all(share, "yhi")
+    u = gathered(both[:, :, :block].sum(axis=0), "z")
 
     scratch = [pltpu.VMEM((held, count), jnp.float32)]
     w, cut_rim = call(
         second_kernel, "second", (full(held, count), full(8, block)), [SMEM] + [VMEM] * 7, scratch, **work
-    )(ids, u, across, *pieces, mix)
+    )(ids, u, both, *pieces, mix)
     u = gathered(summed(w, ROW), ROW)
 
     w = call(third_kernel, "third", full(held, block), [SMEM] + [VMEM] * 7, **work)(
         ids, u, *pieces, row_rim, mix
     )
     share = summed(w, "z")
-    u = gathered(share + swapped(share, "yhi"), "z")
+    u = gathered(from_all(share, "yhi").sum(axis=0), "z")
 
     parts = call(
         fourth_kernel, "fourth", full(2 * peers, half, width), [SMEM] + [VMEM] * 7, scratch, **work

time: 152 us -> 155 us (1.020)
  blocking collectives: 103 us -> 123 us
  starting transfers between devices: 21.9 us -> 12.8 us
  waiting for transfers between devices: 17.3 us -> 9.15 us
    all_to_all x7 -> x9, blocking collectives: 103 us -> 123 us  [exchanged(): return lax.all_to_all(parts, axes, 0, 0, tiled=True)]
    ppermute x3 -> x1, starting transfers between devices: 11.3 us -> 2.15 us  [swapped(): return lax.ppermute(x, axis, [(0, 1), (1, 0)])]
    ppermute x3 -> x1, waiting for transfers between devices: 8.29 us -> 0.19 us  [swapped(): return lax.ppermute(x, axis, [(0, 1), (1, 0)])]
  transfers between devices with their start and end apart: 4 -> 2, of which waited for: 4 -> 2; matrix products, arithmetic and copies ran while one was open for 0% -> 0% of each run, Pallas kernels for 1% -> 1%
where the time goes in v4:
time: 155 us
  blocking collectives  123 us (79%)
  starting transfers between devices  12.8 us (8%)
  waiting for transfers between devices  9.15 us (6%)
  Pallas kernels  7.69 us (5%)
    all_to_all x9, blocking collectives, exchanged(): return lax.all_to_all(parts, axes, 0, 0, tiled=True)  123 us
    all_to_all x1, starting transfers between devices, exchanged(): return lax.all_to_all(parts, axes, 0, 0, tiled=True)  10.6 us
    all_to_all x1, waiting for transfers between devices, exchanged(): return lax.all_to_all(parts, axes, 0, 0, tiled=True)  8.96 us
  transfers between devices with their start and end apart: 2, of which 2 were waited for; matrix products, arithmetic and copies ran while one was open for 0% of the time, Pallas kernels for 1%

profile of v4, /device:TPU:1, one launch (start us, length us, event | category | flops | bytes accessed | tf_op | source)
XLA Modules:
  0.0 154.7 jit_solution(18171130147875935752)
XLA Ops:
  0.0 1.5 pack.1
  1.5 0.0 copy-start
  1.5 0.0 copy-start.1
  1.5 0.0 copy-start.2
  1.5 10.6 %all-to-all-start = ((f32[32,8,384]{2,1,0:T(8,128)}), f32[32,8,384]{2,1,0:T(8,128)S(1)}, u32[]{:S(2)}, u32[]{:S(2)}) async-start(f32[32,8,384]{2,1,0:T(8,128)} %pack.1), calls=%async_computation | async-start | bytes 786432 | tf_op jit(solution)/shard_map/all_to_all | solution.py:30
  12.1 0.0 copy-done
  12.1 2.2 %collective-permute-start = (f32[512,256]{1,0:T(8,128)S(1)}, f32[512,256]{1,0:T(8,128)S(1)}, u32[]{:S(2)}, u32[]{:S(2)}) collective-permute-start(f32[512,256]{1,0:T(8,128)S(1)} %copy-done), channel_id=1, source_target_pairs={{0,16},{16,0},{1,17},{17,1},{2,18},{18,2},{3,19},{19,3},{4,20},{20... | collective-permute-start | bytes 1572872 | tf_op jit(solution)/shard_map/ppermute | solution.py:26
  14.3 0.0 copy-start.3
  14.3 0.1 pad_add_fusion.1.first_ref
  14.4 0.0 copy-done.1
  14.4 0.0 copy-done.2
  14.4 0.6 copy-done.3
  15.0 0.7 mixing.1.mix_ref
  15.7 0.1 pad_add_fusion.ids_ref
  15.7 0.2 collective-permute-done.other_ref
  15.9 0.2 split.1
  16.1 9.0 %all-to-all-done.g_ref = f32[32,8,384]{2,1,0:T(8,128)S(1)} async-done(((f32[32,8,384]{2,1,0:T(8,128)}), f32[32,8,384]{2,1,0:T(8,128)S(1)}, u32[]{:S(2)}, u32[]{:S(2)}) %all-to-all-start) | async-done | bytes 393248 | tf_op jit(solution)/shard_map/all_to_all | solution.py:30
  25.1 1.3 first.1
  26.4 19.3 %all_to_all.50 = f32[8,16,640]{2,1,0:T(8,128)S(1)} all-to-all(f32[8,16,640]{2,1,0:T(8,128)S(1)} %get-tuple-element.17), channel_id=1, replica_groups=mesh['z'=8,'yhi'=2,'core'=2,'x'=4,'ylo'=4] {'z'}, dimensions={0} | all-to-all | bytes 655360 | tf_op jit(solution)/shard_map/all_to_all | solution.py:30
  45.8 10.9 %all_to_all.51.ends_ref = f32[2,16,640]{2,1,0:T(8,128)S(1)} all-to-all(f32[2,16,640]{2,1,0:T(8,128)S(1)} %broadcast_in_dim.10), channel_id=1, replica_groups=mesh['z'=8,'yhi'=2,'core'=2,'x'=4,'ylo'=4] {'yhi'}, dimensions={0} | all-to-all | bytes 163840 | tf_op jit(solution)/shard_map/all_to_all | solution.py:30
  56.7 13.2 %all_to_all.52 = f32[8,16,512]{2,1,0:T(8,128)S(1)} all-to-all(f32[8,16,512]{2,1,0:T(8,128)S(1)} %broadcast_in_dim.11), channel_id=1, replica_groups=mesh['z'=8,'yhi'=2,'core'=2,'x'=4,'ylo'=4] {'z'}, dimensions={0} | all-to-all | bytes 524288 | tf_op jit(solution)/shard_map/all_to_all | solution.py:30
  69.9 1.3 second.1
  71.2 13.0 %all_to_all.53 = f32[16,8,512]{2,1,0:T(8,128)S(1)} all-to-all(f32[16,8,512]{2,1,0:T(8,128)S(1)} %bitcast.21), channel_id=1, replica_groups=mesh['z'=8,'yhi'=2,'core'=2,'x'=4,'ylo'=4] {'x','ylo'}, dimensions={0} | all-to-all | bytes 524288 | tf_op jit(solution)/shard_map/all_to_all | solution.py:30
  84.3 11.0 %all_to_all.54 = f32[16,8,512]{2,1,0:T(8,128)S(1)} all-to-all(f32[16,8,512]{2,1,0:T(8,128)S(1)} %broadcast_in_dim.12), channel_id=1, replica_groups=mesh['z'=8,'yhi'=2,'core'=2,'x'=4,'ylo'=4] {'x','ylo'}, dimensions={0} | all-to-all | bytes 524288 | tf_op jit(solution)/shard_map/all_to_all | solution.py:30
  95.3 1.3 third.1
  96.6 11.7 %all_to_all.55 = f32[8,16,512]{2,1,0:T(8,128)S(1)} all-to-all(f32[8,16,512]{2,1,0:T(8,128)S(1)} %bitcast.19), channel_id=1, replica_groups=mesh['z'=8,'yhi'=2,'core'=2,'x'=4,'ylo'=4] {'z'}, dimensions={0} | all-to-all | bytes 524288 | tf_op jit(solution)/shard_map/all_to_all | solution.py:30
  108.3 9.3 %all_to_all.56 = f32[2,16,512]{2,1,0:T(8,128)S(1)} all-to-all(f32[2,16,512]{2,1,0:T(8,128)S(1)} %broadcast_in_dim.13), channel_id=1, replica_groups=mesh['z'=8,'yhi'=2,'core'=2,'x'=4,'ylo'=4] {'yhi'}, dimensions={0} | all-to-all | bytes 131072 | tf_op jit(solution)/shard_map/all_to_all | solution.py:30
  117.6 11.7 %all_to_all.57 = f32[8,16,512]{2,1,0:T(8,128)S(1)} all-to-all(f32[8,16,512]{2,1,0:T(8,128)S(1)} %broadcast_in_dim.14), channel_id=1, replica_groups=mesh['z'=8,'yhi'=2,'core'=2,'x'=4,'ylo'=4] {'z'}, dimensions={0} | all-to-all | bytes 524288 | tf_op jit(solution)/shard_map/all_to_all | solution.py:30
  129.4 1.3 fourth.1
  130.7 23.4 %all_to_all.58 = f32[32,8,256]{2,1,0:T(8,128)S(1)} all-to-all(f32[32,8,256]{2,1,0:T(8,128)S(1)} %fourth.1), channel_id=1, replica_groups=mesh['z'=8,'yhi'=2,'core'=2,'x'=4,'ylo'=4] {'core','x','ylo'}, dimensions={0} | all-to-all | bytes 524288 | tf_op jit(solution)/shard_map/all_to_all | solution.py:30
  154.1 0.6 bitcast_reduce_fusion
  (10 shorter events, 0.1 us)
Async XLA Ops:
  1.5 10.6 %copy-start = (f32[512,256]{1,0:T(8,128)S(1)}, f32[512,256]{1,0:T(8,128)}, u32[]{:S(2)}) copy-start(f32[512,256]{1,0:T(8,128)} %mine_ref.3) | copy-start | bytes 1572868
  1.5 12.9 %copy-start.1 = (s32[4,8192]{1,0:T(4,128)S(1)}, s32[4,8192]{1,0:T(4,128)}, u32[]{:S(2)}) copy-start(s32[4,8192]{1,0:T(4,128)} %phonon_ref.1) | copy-start | bytes 393220
  1.5 12.9 %copy-start.2 = (s32[4,8192]{1,0:T(4,128)S(1)}, s32[4,8192]{1,0:T(4,128)}, u32[]{:S(2)}) copy-start(s32[4,8192]{1,0:T(4,128)} %fields_ref.1) | copy-start | bytes 393220
  1.5 23.6 %all-to-all-start = ((f32[32,8,384]{2,1,0:T(8,128)}), f32[32,8,384]{2,1,0:T(8,128)S(1)}, u32[]{:S(2)}, u32[]{:S(2)}) async-start(f32[32,8,384]{2,1,0:T(8,128)} %pack.1), calls=%async_computation | async-start | bytes 786432 | tf_op jit(solution)/shard_map/all_to_all | solution.py:30
  12.1 3.8 %collective-permute-start = (f32[512,256]{1,0:T(8,128)S(1)}, f32[512,256]{1,0:T(8,128)S(1)}, u32[]{:S(2)}, u32[]{:S(2)}) collective-permute-start(f32[512,256]{1,0:T(8,128)S(1)} %copy-done), channel_id=1, source_target_pairs={{0,16},{16,0},{1,17},{17,1},{2,18},{18,2},{3,19},{19,3},{4,20},{20... | collective-permute-start | bytes 1572872 | tf_op jit(solution)/shard_map/ppermute | solution.py:26
  14.3 0.7 copy-start.3

commit v5 on v3

--- a/solution.py
+++ b/solution.py
@@ -19,7 +19,6 @@
 PAIRED_ROW = ("core", "x", "ylo")
 
 VMEM = pl.BlockSpec(memory_space=pltpu.VMEM)
-SMEM = pl.BlockSpec(memory_space=pltpu.SMEM)
 
 
 def swapped(x, axis):
@@ -54,17 +53,24 @@
     )
 
 
-def mixing_kernel(first_ref, couplings_ref, phonon_ref, fields_ref, out_ref):
+def place(axes):
+    at = 0
+    for axis in axes:
+        at = at * lax.axis_size(axis) + lax.axis_index(axis)
+    return at
+
+
+def mixing_kernel(block, couplings_ref, phonon_ref, fields_ref, out_ref):
     count = out_ref.shape[2]
     for turn in range(2):
-        first = first_ref[turn]
+        first = place(ROW) * block if turn == 0 else place(CUT) * count
         at_before = pl.ds(pl.multiple_of((first + (SITES - LANES)) % SITES, LANES), LANES)
         at_block = pl.ds(pl.multiple_of(first, LANES), count)
         at_after = pl.ds(pl.multiple_of((first + count) % SITES, LANES), LANES)
         level = jnp.concatenate([phonon_ref[:, at_before], phonon_ref[:, at_block], phonon_ref[:, at_after]], axis=1)
         rate = jnp.zeros(level.shape, jnp.float32)
         for k in range(LEVELS):
-            rate = jnp.where(level == k, couplings_ref[k], rate)
+            rate = jnp.where(level == k, couplings_ref[0:1, k : k + 1], rate)
         grown, shrunk = jnp.exp(rate), jnp.exp(-rate)
         cosh, sinh = 0.5 * (grown + shrunk), 0.5 * (grown - shrunk)
         cosh_left, sinh_left = pltpu.roll(cosh, 1, 1), pltpu.roll(sinh, 1, 1)
@@ -135,8 +141,8 @@
         ref[k : k + 1, :] = row
 
 
-def first_kernel(ids_ref, g_ref, mine_ref, other_ref, mh_ref, ml_ref, oh_ref, ol_ref, mix_ref, out_ref, rim_ref):
-    core, row, z, high = ids_ref[0], ids_ref[1], ids_ref[2], ids_ref[3]
+def first_kernel(g_ref, mine_ref, other_ref, mh_ref, ml_ref, oh_ref, ol_ref, mix_ref, out_ref, rim_ref):
+    core, row, z, high = lax.axis_index("core"), place(ROW), lax.axis_index("z"), lax.axis_index("yhi")
     peers = g_ref.shape[0] // 2
     width = mine_ref.shape[1]
     columns = peers * g_ref.shape[1]
@@ -177,18 +183,18 @@
     return w_ref[...]
 
 
-def second_kernel(ids_ref, u_ref, ends_ref, mh_ref, ml_ref, oh_ref, ol_ref, mix_ref, out_ref, rim_ref, w_ref):
+def second_kernel(u_ref, ends_ref, mh_ref, ml_ref, oh_ref, ol_ref, mix_ref, out_ref, rim_ref, w_ref):
     u = u_ref[...]
-    w = along_product(ids_ref[0], u, mh_ref, ml_ref, oh_ref, ol_ref, w_ref)
+    w = along_product(lax.axis_index("core"), u, mh_ref, ml_ref, oh_ref, ol_ref, w_ref)
     at = u.shape[1]
     rows = [joined([ends_ref[4 * j + k : 4 * j + k + 1, at : at + LANES] for k in range(4)]) for j in range(4)]
     keep_rims(rim_ref, rows)
     out_ref[...] = mixed(w, u, rows, mix_ref[1])
 
 
-def third_kernel(ids_ref, u_ref, mh_ref, ml_ref, oh_ref, ol_ref, rim_ref, mix_ref, out_ref):
+def third_kernel(u_ref, mh_ref, ml_ref, oh_ref, ol_ref, rim_ref, mix_ref, out_ref):
     width = mh_ref.shape[1]
-    core = ids_ref[0]
+    core = lax.axis_index("core")
     u_mine = u_ref[:, pl.ds(pl.multiple_of(core * width, width), width)]
     u_other = u_ref[:, pl.ds(pl.multiple_of((1 - core) * width, width), width)]
     w = product(u_mine, mh_ref, ml_ref, 1) + product(u_other, oh_ref, ol_ref, 1)
@@ -196,9 +202,9 @@
     out_ref[...] = mixed(w, u_ref[...], rows, mix_ref[2])
 
 
-def fourth_kernel(ids_ref, u_ref, mh_ref, ml_ref, oh_ref, ol_ref, rim_ref, mix_ref, out_ref, w_ref):
+def fourth_kernel(u_ref, mh_ref, ml_ref, oh_ref, ol_ref, rim_ref, mix_ref, out_ref, w_ref):
     u = u_ref[...]
-    w = along_product(ids_ref[0], u, mh_ref, ml_ref, oh_ref, ol_ref, w_ref)
+    w = along_product(lax.axis_index("core"), u, mh_ref, ml_ref, oh_ref, ol_ref, w_ref)
     rows = [rim_ref[k : k + 1, :] for k in range(4)]
     f = mixed(w, u, rows, mix_ref[3])
     width = out_ref.shape[2]
@@ -227,39 +233,36 @@
     parts = jnp.broadcast_to(parts[:, None], (2, peers, half, width + LANES))
     g = exchanged(parts.reshape(2 * peers, half, width + LANES), PAIRED_ROW)
 
-    places = ("core", ROW, "z", "yhi")
-    ids = jnp.stack([lax.axis_index(place) for place in places]).astype(jnp.int32)
-    first = jnp.stack([lax.axis_index(ROW) * block, lax.axis_index(CUT) * count]).astype(jnp.int32)
     mix = call(
-        mixing_kernel, "mixing", full(SLICES, 8, count), [SMEM, SMEM, VMEM, VMEM], size=4 * 10 * SITES
-    )(first, couplings, phonon, fields)
+        functools.partial(mixing_kernel, block), "mixing", full(SLICES, 8, count), [VMEM] * 3, size=4 * 10 * SITES
+    )(couplings[None], phonon, fields)
 
     split = jax.ShapeDtypeStruct((block, width), jnp.bfloat16)
     pieces = call(split_kernel, "split", (split,) * 4, [VMEM, VMEM], size=16 * block * width)(mine, other)
 
     work = dict(flops=12 * held * block * count, size=8 * block * count)
     out, row_rim = call(
-        first_kernel, "first", (full(groups, 2 * half, block + LANES), full(8, count)), [SMEM] + [VMEM] * 8, **work
-    )(ids, g, mine, other, *pieces, mix)
+        first_kernel, "first", (full(groups, 2 * half, block + LANES), full(8, count)), [VMEM] * 8, **work
+    )(g, mine, other, *pieces, mix)
     share = exchanged(out, "z").sum(axis=0)
     across = swapped(share, "yhi")
     u = gathered(share[:, :block] + across[:, :block], "z")
 
     scratch = [pltpu.VMEM((held, count), jnp.float32)]
     w, cut_rim = call(
-        second_kernel, "second", (full(held, count), full(8, block)), [SMEM] + [VMEM] * 7, scratch, **work
-    )(ids, u, across, *pieces, mix)
+        second_kernel, "second", (full(held, count), full(8, block)), [VMEM] * 7, scratch, **work
+    )(u, across, *pieces, mix)
     u = gathered(summed(w, ROW), ROW)
 
-    w = call(third_kernel, "third", full(held, block), [SMEM] + [VMEM] * 7, **work)(
-        ids, u, *pieces, row_rim, mix
+    w = call(third_kernel, "third", full(held, block), [VMEM] * 7, **work)(
+        u, *pieces, row_rim, mix
     )
     share = summed(w, "z")
     u = gathered(share + swapped(share, "yhi"), "z")
 
     parts = call(
-        fourth_kernel, "fourth", full(2 * peers, half, width), [SMEM] + [VMEM] * 7, scratch, **work
-    )(ids, u, *pieces, cut_rim, mix)
+        fourth_kernel, "fourth", full(2 * peers, half, width), [VMEM] * 7, scratch, **work
+    )(u, *pieces, cut_rim, mix)
     out = exchanged(parts, PAIRED_ROW).reshape(2, peers, half, width).sum(axis=1)
     return out.reshape(2 * half, width).T
 

time: 152 us -> 150 us (0.987)
  Pallas kernels: 6.19 us -> 3.41 us
  waiting for transfers between devices: 17.3 us -> 19.5 us
    pallas_call x4, Pallas kernels: 4.66 us -> 2.43 us  [the longest x1 0.77 us: shards(): call(third_kernel, 'third', full(held, block), [VMEM] * 7, **work)]
    ppermute x3, waiting for transfers between devices: 8.29 us -> 10.5 us  [swapped(): return lax.ppermute(x, axis, [(0, 1), (1, 0)])]
  transfers between devices with their start and end apart: 4 -> 4, of which waited for: 4 -> 4; matrix products, arithmetic and copies ran while one was open for 0% -> 0% of each run, Pallas kernels for 1% -> 0%
where the time goes in v5:
time: 150 us; the launch traced here: 149 us
  blocking collectives  103 us (69%)
  starting transfers between devices  20.8 us (14%)
  waiting for transfers between devices  19.5 us (13%)
  Pallas kernels  3.41 us (2%)
  local copies, waits for them, and re-layouts  1.62 us (1%)
    all_to_all x7, blocking collectives, exchanged(): return lax.all_to_all(parts, axes, 0, 0, tiled=True)  103 us
    all_to_all x1, starting transfers between devices, exchanged(): return lax.all_to_all(parts, axes, 0, 0, tiled=True)  10.6 us
    ppermute x3, waiting for transfers between devices, swapped(): return lax.ppermute(x, axis, [(0, 1), (1, 0)])  10.5 us
    ppermute x3, starting transfers between devices, swapped(): return lax.ppermute(x, axis, [(0, 1), (1, 0)])  10.2 us
    all_to_all x1, waiting for transfers between devices, exchanged(): return lax.all_to_all(parts, axes, 0, 0, tiled=True)  8.95 us
  transfers between devices with their start and end apart: 4, of which 4 were waited for; matrix products, arithmetic and copies ran while one was open for 0% of the time, Pallas kernels for 0%

profile of v5, /device:TPU:1, one launch (start us, length us, event | category | flops | bytes accessed | tf_op | source)
XLA Modules:
  0.0 149.2 jit_solution(15436687768305630302)
XLA Ops:
  0.0 0.0 copy-start.4
  0.0 0.7 fusion.2
  0.8 0.0 copy-done.4
  0.8 0.0 copy-start
  0.8 0.8 broadcast_in_dim.10
  1.6 0.0 copy-start.1
  1.6 0.0 copy-start.2
  1.6 10.6 %all-to-all-start = ((f32[32,8,384]{2,1,0:T(8,128)}), f32[32,8,384]{2,1,0:T(8,128)S(1)}, u32[]{:S(2)}, u32[]{:S(2)}) async-start(f32[32,8,384]{2,1,0:T(8,128)} %bitcast.3), calls=%async_computation | async-start | bytes 786432 | tf_op jit(solution)/shard_map/all_to_all | solution.py:29
  12.2 0.0 copy-done
  12.2 0.0 copy-start.3
  12.2 2.2 %collective-permute-start = (f32[512,256]{1,0:T(8,128)S(1)}, f32[512,256]{1,0:T(8,128)S(1)}, u32[]{:S(2)}, u32[]{:S(2)}) collective-permute-start(f32[512,256]{1,0:T(8,128)S(1)} %copy-done), channel_id=1, source_target_pairs={{0,16},{16,0},{1,17},{17,1},{2,18},{18,2},{3,19},{19,3},{4,20},{20... | collective-permute-start | bytes 1572872 | tf_op jit(solution)/shard_map/ppermute | solution.py:25
  14.4 0.0 copy-done.1
  14.4 0.0 copy-done.2
  14.4 0.0 copy-done.3
  14.4 0.2 mixing.1.mix_ref
  14.6 1.4 collective-permute-done.other_ref
  16.0 0.2 split.1
  16.2 8.9 %all-to-all-done.g_ref = f32[32,8,384]{2,1,0:T(8,128)S(1)} async-done(((f32[32,8,384]{2,1,0:T(8,128)}), f32[32,8,384]{2,1,0:T(8,128)S(1)}, u32[]{:S(2)}, u32[]{:S(2)}) %all-to-all-start) | async-done | bytes 393248 | tf_op jit(solution)/shard_map/all_to_all | solution.py:29
  25.2 0.8 first.1
  26.0 19.3 %all_to_all.40 = f32[8,16,640]{2,1,0:T(8,128)S(1)} all-to-all(f32[8,16,640]{2,1,0:T(8,128)S(1)} %get-tuple-element.17), channel_id=1, replica_groups=mesh['z'=8,'yhi'=2,'core'=2,'x'=4,'ylo'=4] {'z'}, dimensions={0} | all-to-all | bytes 655360 | tf_op jit(solution)/shard_map/all_to_all | solution.py:29
  45.3 4.8 %collective-permute-start.1 = (f32[16,640]{1,0:T(8,128)S(1)}, f32[16,640]{1,0:T(8,128)S(1)}, u32[]{:S(2)}, u32[]{:S(2)}) collective-permute-start(f32[16,640]{1,0:T(8,128)S(1)} %reduce_sum.36), channel_id=1, source_target_pairs={{0,32},{32,0},{1,33},{33,1},{2,34},{34,2},{3,35},{35,3},{4,36},{36... | collective-permute-start | bytes 122888 | tf_op jit(solution)/shard_map/ppermute | solution.py:25
  50.1 3.9 %collective-permute-done.1.ends_ref = f32[16,640]{1,0:T(8,128)S(1)} collective-permute-done((f32[16,640]{1,0:T(8,128)S(1)}, f32[16,640]{1,0:T(8,128)S(1)}, u32[]{:S(2)}, u32[]{:S(2)}) %collective-permute-start.1) | collective-permute-done | bytes 40992 | tf_op jit(solution)/shard_map/ppermute | solution.py:25
  54.0 12.7 %all_to_all.41 = f32[8,16,512]{2,1,0:T(8,128)S(1)} all-to-all(f32[8,16,512]{2,1,0:T(8,128)S(1)} %broadcast_in_dim.12), channel_id=1, replica_groups=mesh['z'=8,'yhi'=2,'core'=2,'x'=4,'ylo'=4] {'z'}, dimensions={0} | all-to-all | bytes 524288 | tf_op jit(solution)/shard_map/all_to_all | solution.py:29
  66.7 0.7 second.1
  67.5 13.5 %all_to_all.42 = f32[16,8,512]{2,1,0:T(8,128)S(1)} all-to-all(f32[16,8,512]{2,1,0:T(8,128)S(1)} %bitcast.21), channel_id=1, replica_groups=mesh['z'=8,'yhi'=2,'core'=2,'x'=4,'ylo'=4] {'x','ylo'}, dimensions={0} | all-to-all | bytes 524288 | tf_op jit(solution)/shard_map/all_to_all | solution.py:29
  81.0 10.9 %all_to_all.43 = f32[16,8,512]{2,1,0:T(8,128)S(1)} all-to-all(f32[16,8,512]{2,1,0:T(8,128)S(1)} %broadcast_in_dim.13), channel_id=1, replica_groups=mesh['z'=8,'yhi'=2,'core'=2,'x'=4,'ylo'=4] {'x','ylo'}, dimensions={0} | all-to-all | bytes 524288 | tf_op jit(solution)/shard_map/all_to_all | solution.py:29
  92.0 0.8 third.1
  92.8 13.5 %all_to_all.44 = f32[8,16,512]{2,1,0:T(8,128)S(1)} all-to-all(f32[8,16,512]{2,1,0:T(8,128)S(1)} %bitcast.19), channel_id=1, replica_groups=mesh['z'=8,'yhi'=2,'core'=2,'x'=4,'ylo'=4] {'z'}, dimensions={0} | all-to-all | bytes 524288 | tf_op jit(solution)/shard_map/all_to_all | solution.py:29
  106.3 3.3 %collective-permute-start.2 = (f32[16,512]{1,0:T(8,128)S(1)}, f32[16,512]{1,0:T(8,128)S(1)}, u32[]{:S(2)}, u32[]{:S(2)}) collective-permute-start(f32[16,512]{1,0:T(8,128)S(1)} %reduce_sum.38), channel_id=1, source_target_pairs={{0,32},{32,0},{1,33},{33,1},{2,34},{34,2},{3,35},{35,3},{4,36},{36... | collective-permute-start | bytes 98312 | tf_op jit(solution)/shard_map/ppermute | solution.py:25
  109.6 5.2 %collective-permute-done.2 = f32[16,512]{1,0:T(8,128)S(1)} collective-permute-done((f32[16,512]{1,0:T(8,128)S(1)}, f32[16,512]{1,0:T(8,128)S(1)}, u32[]{:S(2)}, u32[]{:S(2)}) %collective-permute-start.2) | collective-permute-done | bytes 32800 | tf_op jit(solution)/shard_map/ppermute | solution.py:25
  114.9 11.7 %all_to_all.45 = f32[8,16,512]{2,1,0:T(8,128)S(1)} all-to-all(f32[8,16,512]{2,1,0:T(8,128)S(1)} %broadcast_in_dim.14), channel_id=1, replica_groups=mesh['z'=8,'yhi'=2,'core'=2,'x'=4,'ylo'=4] {'z'}, dimensions={0} | all-to-all | bytes 524288 | tf_op jit(solution)/shard_map/all_to_all | solution.py:29
  126.6 0.7 fourth.1
  127.4 21.3 %all_to_all.46 = f32[32,8,256]{2,1,0:T(8,128)S(1)} all-to-all(f32[32,8,256]{2,1,0:T(8,128)S(1)} %fourth.1), channel_id=1, replica_groups=mesh['z'=8,'yhi'=2,'core'=2,'x'=4,'ylo'=4] {'core','x','ylo'}, dimensions={0} | all-to-all | bytes 524288 | tf_op jit(solution)/shard_map/all_to_all | solution.py:29
  148.6 0.6 bitcast_reduce_fusion
  (13 shorter events, 0.2 us)
Async XLA Ops:
  0.0 0.8 copy-start.4
  0.8 11.4 %copy-start = (f32[512,256]{1,0:T(8,128)S(1)}, f32[512,256]{1,0:T(8,128)}, u32[]{:S(2)}) copy-start(f32[512,256]{1,0:T(8,128)} %mine_ref.3) | copy-start | bytes 1572868
  1.6 12.8 %copy-start.1 = (s32[4,8192]{1,0:T(4,128)S(1)}, s32[4,8192]{1,0:T(4,128)}, u32[]{:S(2)}) copy-start(s32[4,8192]{1,0:T(4,128)} %phonon_ref.1) | copy-start | bytes 393220
  1.6 12.8 %copy-start.2 = (s32[4,8192]{1,0:T(4,128)S(1)}, s32[4,8192]{1,0:T(4,128)}, u32[]{:S(2)}) copy-start(s32[4,8192]{1,0:T(4,128)} %fields_ref.1) | copy-start | bytes 393220
  1.6 23.6 %all-to-all-start = ((f32[32,8,384]{2,1,0:T(8,128)}), f32[32,8,384]{2,1,0:T(8,128)S(1)}, u32[]{:S(2)}, u32[]{:S(2)}) async-start(f32[32,8,384]{2,1,0:T(8,128)} %bitcast.3), calls=%async_computation | async-start | bytes 786432 | tf_op jit(solution)/shard_map/all_to_all | solution.py:29
  12.2 2.2 %copy-start.3 = (f32[16]{0:T(128)S(1)}, f32[16]{0:T(128)}, u32[]{:S(2)}) copy-start(f32[16]{0:T(128)} %param.9) | copy-start | bytes 196
  12.2 3.8 %collective-permute-start = (f32[512,256]{1,0:T(8,128)S(1)}, f32[512,256]{1,0:T(8,128)S(1)}, u32[]{:S(2)}, u32[]{:S(2)}) collective-permute-start(f32[512,256]{1,0:T(8,128)S(1)} %copy-done), channel_id=1, source_target_pairs={{0,16},{16,0},{1,17},{17,1},{2,18},{18,2},{3,19},{19,3},{4,20},{20... | collective-permute-start | bytes 1572872 | tf_op jit(solution)/shard_map/ppermute | solution.py:25
  45.3 8.7 %collective-permute-start.1 = (f32[16,640]{1,0:T(8,128)S(1)}, f32[16,640]{1,0:T(8,128)S(1)}, u32[]{:S(2)}, u32[]{:S(2)}) collective-permute-start(f32[16,640]{1,0:T(8,128)S(1)} %reduce_sum.36), channel_id=1, source_target_pairs={{0,32},{32,0},{1,33},{33,1},{2,34},{34,2},{3,35},{35,3},{4,36},{36... | collective-permute-start | bytes 122888 | tf_op jit(solution)/shard_map/ppermute | solution.py:25
  106.3 8.6 %collective-permute-start.2 = (f32[16,512]{1,0:T(8,128)S(1)}, f32[16,512]{1,0:T(8,128)S(1)}, u32[]{:S(2)}, u32[]{:S(2)}) collective-permute-start(f32[16,512]{1,0:T(8,128)S(1)} %reduce_sum.38), channel_id=1, source_target_pairs={{0,32},{32,0},{1,33},{33,1},{2,34},{34,2},{3,35},{35,3},{4,36},{36... | collective-permute-start | bytes 98312 | tf_op jit(solution)/shard_map/ppermute | solution.py:25

commit v6 on v5

--- a/solution.py
+++ b/solution.py
@@ -258,7 +258,7 @@
         u, *pieces, row_rim, mix
     )
     share = summed(w, "z")
-    u = gathered(share + swapped(share, "yhi"), "z")
+    u = gathered(share, CUT).reshape(groups, 2, 2 * half, block).sum(axis=1).reshape(held, block)
 
     parts = call(
         fourth_kernel, "fourth", full(2 * peers, half, width), [VMEM] * 7, scratch, **work

time: 150 us -> 149 us (level)
  blocking collectives: 103 us -> 111 us
  waiting for transfers between devices: 19.5 us -> 14.2 us
  starting transfers between devices: 20.8 us -> 17.5 us
    all_to_all x7, blocking collectives: 103 us -> 111 us  [exchanged(): return lax.all_to_all(parts, axes, 0, 0, tiled=True)]
    ppermute x3 -> x2, waiting for transfers between devices: 10.5 us -> 5.26 us  [swapped(): return lax.ppermute(x, axis, [(0, 1), (1, 0)])]
    ppermute x3 -> x2, starting transfers between devices: 10.2 us -> 6.91 us  [swapped(): return lax.ppermute(x, axis, [(0, 1), (1, 0)])]
  transfers between devices with their start and end apart: 4 -> 3, of which waited for: 4 -> 3; matrix products, arithmetic and copies ran while one was open for 0% -> 0% of each run, Pallas kernels for 0% -> 0%
where the time goes in v6:
time: 149 us; the launch traced here: 148 us
  blocking collectives  111 us (74%)
  starting transfers between devices  17.5 us (12%)
  waiting for transfers between devices  14.2 us (10%)
  Pallas kernels  3.41 us (2%)
  local copies, waits for them, and re-layouts  1.63 us (1%)
    all_to_all x7, blocking collectives, exchanged(): return lax.all_to_all(parts, axes, 0, 0, tiled=True)  111 us
    all_to_all x1, starting transfers between devices, exchanged(): return lax.all_to_all(parts, axes, 0, 0, tiled=True)  10.6 us
    all_to_all x1, waiting for transfers between devices, exchanged(): return lax.all_to_all(parts, axes, 0, 0, tiled=True)  8.95 us
    ppermute x2, starting transfers between devices, swapped(): return lax.ppermute(x, axis, [(0, 1), (1, 0)])  6.91 us
    ppermute x2, waiting for transfers between devices, swapped(): return lax.ppermute(x, axis, [(0, 1), (1, 0)])  5.26 us
  transfers between devices with their start and end apart: 3, of which 3 were waited for; matrix products, arithmetic and copies ran while one was open for 0% of the time, Pallas kernels for 0%

profile of v6, /device:TPU:1, one launch (start us, length us, event | category | flops | bytes accessed | tf_op | source)
XLA Modules:
  0.0 148.2 jit_solution(8413104796806758220)
XLA Ops:
  0.0 0.0 copy-start.4
  0.0 0.7 fusion.2
  0.8 0.0 copy-done.4
  0.8 0.0 copy-start
  0.8 0.8 broadcast_in_dim.10
  1.6 0.0 copy-start.1
  1.6 0.0 copy-start.2
  1.6 10.6 %all-to-all-start = ((f32[32,8,384]{2,1,0:T(8,128)}), f32[32,8,384]{2,1,0:T(8,128)S(1)}, u32[]{:S(2)}, u32[]{:S(2)}) async-start(f32[32,8,384]{2,1,0:T(8,128)} %bitcast.3), calls=%async_computation | async-start | bytes 786432 | tf_op jit(solution)/shard_map/all_to_all | solution.py:29
  12.2 0.0 copy-done
  12.2 0.0 copy-start.3
  12.2 2.2 %collective-permute-start = (f32[512,256]{1,0:T(8,128)S(1)}, f32[512,256]{1,0:T(8,128)S(1)}, u32[]{:S(2)}, u32[]{:S(2)}) collective-permute-start(f32[512,256]{1,0:T(8,128)S(1)} %copy-done), channel_id=1, source_target_pairs={{0,16},{16,0},{1,17},{17,1},{2,18},{18,2},{3,19},{19,3},{4,20},{20... | collective-permute-start | bytes 1572872 | tf_op jit(solution)/shard_map/ppermute | solution.py:25
  14.4 0.0 copy-done.1
  14.4 0.0 copy-done.2
  14.4 0.0 copy-done.3
  14.4 0.2 mixing.1.mix_ref
  14.6 1.4 collective-permute-done.other_ref
  16.0 0.2 split.1
  16.2 8.9 %all-to-all-done.g_ref = f32[32,8,384]{2,1,0:T(8,128)S(1)} async-done(((f32[32,8,384]{2,1,0:T(8,128)}), f32[32,8,384]{2,1,0:T(8,128)S(1)}, u32[]{:S(2)}, u32[]{:S(2)}) %all-to-all-start) | async-done | bytes 393248 | tf_op jit(solution)/shard_map/all_to_all | solution.py:29
  25.1 0.8 first.1
  25.9 19.3 %all_to_all.40 = f32[8,16,640]{2,1,0:T(8,128)S(1)} all-to-all(f32[8,16,640]{2,1,0:T(8,128)S(1)} %get-tuple-element.17), channel_id=1, replica_groups=mesh['z'=8,'yhi'=2,'core'=2,'x'=4,'ylo'=4] {'z'}, dimensions={0} | all-to-all | bytes 655360 | tf_op jit(solution)/shard_map/all_to_all | solution.py:29
  45.3 4.8 %collective-permute-start.1 = (f32[16,640]{1,0:T(8,128)S(1)}, f32[16,640]{1,0:T(8,128)S(1)}, u32[]{:S(2)}, u32[]{:S(2)}) collective-permute-start(f32[16,640]{1,0:T(8,128)S(1)} %reduce_sum.45), channel_id=1, source_target_pairs={{0,32},{32,0},{1,33},{33,1},{2,34},{34,2},{3,35},{35,3},{4,36},{36... | collective-permute-start | bytes 122888 | tf_op jit(solution)/shard_map/ppermute | solution.py:25
  50.1 3.9 %collective-permute-done.1.ends_ref = f32[16,640]{1,0:T(8,128)S(1)} collective-permute-done((f32[16,640]{1,0:T(8,128)S(1)}, f32[16,640]{1,0:T(8,128)S(1)}, u32[]{:S(2)}, u32[]{:S(2)}) %collective-permute-start.1) | collective-permute-done | bytes 40992 | tf_op jit(solution)/shard_map/ppermute | solution.py:25
  54.0 12.7 %all_to_all.41 = f32[8,16,512]{2,1,0:T(8,128)S(1)} all-to-all(f32[8,16,512]{2,1,0:T(8,128)S(1)} %broadcast_in_dim.12), channel_id=1, replica_groups=mesh['z'=8,'yhi'=2,'core'=2,'x'=4,'ylo'=4] {'z'}, dimensions={0} | all-to-all | bytes 524288 | tf_op jit(solution)/shard_map/all_to_all | solution.py:29
  66.7 0.7 second.1
  67.5 13.5 %all_to_all.42 = f32[16,8,512]{2,1,0:T(8,128)S(1)} all-to-all(f32[16,8,512]{2,1,0:T(8,128)S(1)} %bitcast.23), channel_id=1, replica_groups=mesh['z'=8,'yhi'=2,'core'=2,'x'=4,'ylo'=4] {'x','ylo'}, dimensions={0} | all-to-all | bytes 524288 | tf_op jit(solution)/shard_map/all_to_all | solution.py:29
  81.0 10.9 %all_to_all.43 = f32[16,8,512]{2,1,0:T(8,128)S(1)} all-to-all(f32[16,8,512]{2,1,0:T(8,128)S(1)} %broadcast_in_dim.13), channel_id=1, replica_groups=mesh['z'=8,'yhi'=2,'core'=2,'x'=4,'ylo'=4] {'x','ylo'}, dimensions={0} | all-to-all | bytes 524288 | tf_op jit(solution)/shard_map/all_to_all | solution.py:29
  92.0 0.8 third.1
  92.7 13.4 %all_to_all.44 = f32[8,16,512]{2,1,0:T(8,128)S(1)} all-to-all(f32[8,16,512]{2,1,0:T(8,128)S(1)} %bitcast.21), channel_id=1, replica_groups=mesh['z'=8,'yhi'=2,'core'=2,'x'=4,'ylo'=4] {'z'}, dimensions={0} | all-to-all | bytes 524288 | tf_op jit(solution)/shard_map/all_to_all | solution.py:29
  106.2 0.1 broadcast_in_dim.14
  106.3 16.4 %all_to_all.45 = f32[16,16,512]{2,1,0:T(8,128)S(1)} all-to-all(f32[16,16,512]{2,1,0:T(8,128)S(1)} %broadcast_in_dim.14), channel_id=1, replica_groups=mesh['z'=8,'yhi'=2,'core'=2,'x'=4,'ylo'=4] {'z','yhi'}, dimensions={0} | all-to-all | bytes 1048576 | tf_op jit(solution)/shard_map/all_to_all | solution.py:29
  122.7 0.7 fourth.1
  123.5 24.1 %all_to_all.46 = f32[32,8,256]{2,1,0:T(8,128)S(1)} all-to-all(f32[32,8,256]{2,1,0:T(8,128)S(1)} %fourth.1), channel_id=1, replica_groups=mesh['z'=8,'yhi'=2,'core'=2,'x'=4,'ylo'=4] {'core','x','ylo'}, dimensions={0} | all-to-all | bytes 524288 | tf_op jit(solution)/shard_map/all_to_all | solution.py:29
  147.6 0.6 bitcast_reduce_fusion.1
  (12 shorter events, 0.2 us)
Async XLA Ops:
  0.0 0.8 copy-start.4
  0.8 11.4 %copy-start = (f32[512,256]{1,0:T(8,128)S(1)}, f32[512,256]{1,0:T(8,128)}, u32[]{:S(2)}) copy-start(f32[512,256]{1,0:T(8,128)} %mine_ref.3) | copy-start | bytes 1572868
  1.6 12.8 %copy-start.1 = (s32[4,8192]{1,0:T(4,128)S(1)}, s32[4,8192]{1,0:T(4,128)}, u32[]{:S(2)}) copy-start(s32[4,8192]{1,0:T(4,128)} %phonon_ref.1) | copy-start | bytes 393220
  1.6 12.8 %copy-start.2 = (s32[4,8192]{1,0:T(4,128)S(1)}, s32[4,8192]{1,0:T(4,128)}, u32[]{:S(2)}) copy-start(s32[4,8192]{1,0:T(4,128)} %fields_ref.1) | copy-start | bytes 393220
  1.6 23.6 %all-to-all-start = ((f32[32,8,384]{2,1,0:T(8,128)}), f32[32,8,384]{2,1,0:T(8,128)S(1)}, u32[]{:S(2)}, u32[]{:S(2)}) async-start(f32[32,8,384]{2,1,0:T(8,128)} %bitcast.3), calls=%async_computation | async-start | bytes 786432 | tf_op jit(solution)/shard_map/all_to_all | solution.py:29
  12.2 2.2 %copy-start.3 = (f32[16]{0:T(128)S(1)}, f32[16]{0:T(128)}, u32[]{:S(2)}) copy-start(f32[16]{0:T(128)} %param.9) | copy-start | bytes 196
  12.2 3.8 %collective-permute-start = (f32[512,256]{1,0:T(8,128)S(1)}, f32[512,256]{1,0:T(8,128)S(1)}, u32[]{:S(2)}, u32[]{:S(2)}) collective-permute-start(f32[512,256]{1,0:T(8,128)S(1)} %copy-done), channel_id=1, source_target_pairs={{0,16},{16,0},{1,17},{17,1},{2,18},{18,2},{3,19},{19,3},{4,20},{20... | collective-permute-start | bytes 1572872 | tf_op jit(solution)/shard_map/ppermute | solution.py:25
  45.3 8.7 %collective-permute-start.1 = (f32[16,640]{1,0:T(8,128)S(1)}, f32[16,640]{1,0:T(8,128)S(1)}, u32[]{:S(2)}, u32[]{:S(2)}) collective-permute-start(f32[16,640]{1,0:T(8,128)S(1)} %reduce_sum.45), channel_id=1, source_target_pairs={{0,32},{32,0},{1,33},{33,1},{2,34},{34,2},{3,35},{35,3},{4,36},{36... | collective-permute-start | bytes 122888 | tf_op jit(solution)/shard_map/ppermute | solution.py:25
